TPU v7x, 256 devices: a whole 4x4x8 slice. The times are simulated.
256 devices in a mesh: rows: 32 (over z, x), tp: 4 (over y), unit: 2 (over core).
Axes of the slice: x: 4, y: 4, z: 8, core: 2. Of those that a mesh axis runs over, the one named last changes fastest.
Arguments:
- train_query: bfloat16 [4096, 2048], P(('unit', 'rows'), 'tp'), parts along dimension 0, may hold values from -0.125 to 0.125
- low_query: bfloat16 [4096, 64], P(('unit', 'rows')), parts along dimension 0, may hold values from -0.125 to 0.125
- high_query: bfloat16 [128, 2048], P('unit', 'tp'), parts along dimension 0, may hold values from -0.75 to 0.75
- train_key: bfloat16 [4096, 512], P(('unit', 'rows'), 'tp'), parts along dimension 0, may hold values from -0.125 to 0.125
- low_key: bfloat16 [4096, 64], P(('unit', 'rows')), parts along dimension 0, may hold values from -0.125 to 0.125
- high_key: bfloat16 [128, 512], P('unit', 'tp'), parts along dimension 0, may hold values from -0.75 to 0.75
- train_value: bfloat16 [4096, 512], P(('unit', 'rows'), 'tp'), parts along dimension 0, may hold values from -0.125 to 0.125
- low_value: bfloat16 [4096, 64], P(('unit', 'rows')), parts along dimension 0, may hold values from -0.125 to 0.125
- high_value: bfloat16 [128, 512], P('unit', 'tp'), parts along dimension 0, may hold values from -0.75 to 0.75
- norm_train: float32 [4096], P(('unit', 'rows', 'tp')), parts along dimension 0, may hold values from 0.25 to 1.75
- norm_step: float32 [4096], P(('unit', 'rows', 'tp')), parts along dimension 0, may hold values from -0.3 to 0.3
Outputs:
- final_query: bfloat16 [4096, 2048], P(('unit', 'tp')), parts along dimension 0
- final_key: bfloat16 [1024, 2048], P(('unit', 'tp')), parts along dimension 0
- final_value: bfloat16 [1024, 2048], P(('unit', 'tp')), parts along dimension 0
- serve_norm: bfloat16 [4096], P('unit'), parts along dimension 0
There are 2 independent parts, one for each index of `unit`. A program takes and returns all parts, laid end to end along the dimension named above; each array names one. Nothing has to cross between parts.
All inputs are finite; a program needn't handle non-finite values.
Results may differ from a plain program's by a relative error of at most 0.001.
Values may be sent and summed in bfloat16 or wider, within the bound.
No kernel may reach another device: no remote copies, remote signals or barrier semaphores. Data moves between devices by JAX's collectives and lax.ppermute only.
A program may use at most 64 MiB of HBM per device.

v0:
```python
import jax
import jax.numpy as jnp
from jax import lax
from jax.experimental import pallas as pl
from jax.experimental.pallas import tpu as pltpu
from jax.sharding import Mesh
from jax.sharding import PartitionSpec as P

ROWS = ("rows_0", "rows_1")
UNIT_ROWS = ("unit", "rows_0", "rows_1")
UNIT_ROWS_TP = ("unit", "rows_0", "rows_1", "tp")
RING_0, RING_1, TP = 8, 4, 4
RANKS = RING_0 * RING_1

mix_rate = 0.5

LANES = 128
BLOCK = 64
CHUNKS = 6
WEIGHT_ROWS = CHUNKS * BLOCK
SENT_ROWS = WEIGHT_ROWS + 8

STEPS = (
    ((4, 0), ((0, 0),)),
    ((0, 2), ((0, 0),)),
    ((2, 0), ((0, 0),)),
    ((6, 0), ((0, 0),)),
    ((-1, 0), ((0, 0), (0, 2))),
    ((0, -1), ((4, 0),)),
    ((1, 0), ((0, 0), (0, 2), (4, 0))),
    ((0, 1), ((4, 0),)),
    ((0, -1), ((2, 0), (4, 3))),
    ((0, 1), ((0, 0), (2, 0), (6, 0))),
    ((-1, 0), ((4, 1), (4, 3))),
    ((1, 0), ((2, 0), (4, 3))),
    ((0, -1), ((0, 0), (6, 0), (7, 2), (7, 0))),
    ((-1, 0), ((2, 3), (4, 2), (7, 2))),
    ((0, 1), ((1, 0), (5, 0))),
    ((1, 0), ((1, 2), (4, 2))),
)


def from_offset(array, dz, dx):
    pairs = []
    for z in range(RING_0):
        for x in range(RING_1):
            source = (z + dz) % RING_0 * RING_1 + (x + dx) % RING_1
            pairs.append((source, z * RING_1 + x))
    return lax.ppermute(array, ROWS, pairs)


def merge_kernel(tq, lq, hq, tk, lk, hk, tv, lv, hv, out):
    chunk = 0
    for train, low, high in ((tq, lq, hq), (tk, lk, hk), (tv, lv, hv)):
        result = train[...].astype(jnp.float32) + mix_rate * jnp.dot(
            low[...], high[...], preferred_element_type=jnp.float32
        )
        result = result.astype(jnp.bfloat16)
        for at in range(0, result.shape[1], LANES):
            out[chunk * BLOCK : (chunk + 1) * BLOCK, :] = result[:, at : at + LANES]
            chunk += 1
    out[WEIGHT_ROWS:, :] = jnp.zeros((SENT_ROWS - WEIGHT_ROWS, LANES), jnp.bfloat16)


def gain_kernel(_, own, first, second, third, out):
    out[WEIGHT_ROWS:, :] = own[...] + first[...] + second[...] + third[...]


def place_kernel(pieces, *refs):
    n = 1 + max(p[0] for p in pieces)
    sent, (query, key, value, norm), (rows, tiles, turned, sems) = refs[:n], refs[n : n + 4], refs[n + 4 :]
    z, x = lax.axis_index("rows_0"), lax.axis_index("rows_1")
    for at, row, (dz, dx) in pieces:
        rank = lax.rem(z + dz % RING_0, RING_0) * RING_1 + lax.rem(x + dx % RING_1, RING_1)
        start = pl.multiple_of(rank * BLOCK, BLOCK)
        for chunk in range(CHUNKS):
            rows[chunk, pl.ds(start, BLOCK), :] = sent[at][row + chunk * BLOCK : row + (chunk + 1) * BLOCK, :]
        tiles[rank] = sent[at][row + WEIGHT_ROWS : row + SENT_ROWS, :].astype(jnp.float32)
    lane = lax.broadcasted_iota(jnp.int32, (1, LANES), 1)
    for pair in range(RANKS // 2):
        both = jnp.where(lane < BLOCK, tiles[2 * pair, 0:1, :], tiles[2 * pair + 1, 0:1, :])
        norm[pair : pair + 1, :] = both.astype(jnp.bfloat16)
    copies = []
    for chunk in range(CHUNKS):
        for tile in range(RANKS * BLOCK // LANES):
            lanes = slice(tile * LANES, (tile + 1) * LANES)
            turned[chunk, :, lanes] = rows[chunk, lanes, :].T
        out, row = ((query, chunk), (key, chunk - 4), (value, chunk - 5))[max(0, chunk - 3)]
        copies.append(
            pltpu.make_async_copy(turned.at[chunk], out.at[row * LANES : (row + 1) * LANES, :], sems.at[chunk])
        )
        copies[-1].start()
    for copy in copies:
        copy.wait()


def shards(
    train_query,
    low_query,
    high_query,
    train_key,
    low_key,
    high_key,
    train_value,
    low_value,
    high_value,
    norm_train,
    norm_step,
):
    bf16, vmem = jnp.bfloat16, pl.BlockSpec(memory_space=pltpu.VMEM)
    gain = jnp.tile((norm_train + norm_step).astype(bf16), LANES // 16)
    own = lax.broadcasted_iota(jnp.int32, (8, LANES), 1) // 16 % TP == lax.axis_index("tp")
    gain = jnp.where(own, gain[None, :], jnp.zeros((), bf16))
    others = [lax.ppermute(gain, "tp", [(i, (i + s) % TP) for i in range(TP)]) for s in range(1, TP)]
    block = pl.pallas_call(
        merge_kernel,
        out_shape=pltpu.VMEM((SENT_ROWS, LANES), bf16),
        in_specs=[vmem] * 9,
        out_specs=vmem,
        name="merge",
    )(train_query, low_query, high_query, train_key, low_key, high_key, train_value, low_value, high_value)
    block = pl.pallas_call(
        gain_kernel,
        out_shape=pltpu.VMEM((SENT_ROWS, LANES), bf16),
        in_specs=[vmem] * 5,
        out_specs=vmem,
        input_output_aliases={0: 0},
        name="gain",
    )(*(pltpu.with_memory_space_constraint(a, pltpu.VMEM) for a in (block, gain, *others)))

    sent, held = [block], {(0, 0): (0, 0)}
    for offset, passed in STEPS:
        parts = [sent[at][row : row + SENT_ROWS] for at, row in (held[p] for p in passed)]
        arrived = from_offset(parts[0] if len(parts) == 1 else jnp.concatenate(parts, axis=0), *offset)
        for place, (dz, dx) in enumerate(passed):
            held[(offset[0] + dz) % RING_0, (offset[1] + dx) % RING_1] = (len(sent), place * SENT_ROWS)
        sent.append(arrived)
    pieces = [(at, row, offset) for offset, (at, row) in held.items()]
    assert len(pieces) == RANKS == 1 + sum(len(passed) for _, passed in STEPS)

    hbm = pl.BlockSpec(memory_space=pl.ANY)
    width = RANKS * BLOCK
    query, key, value, norm = pl.pallas_call(
        lambda *refs: place_kernel(pieces, *refs),
        out_shape=(
            jax.ShapeDtypeStruct((4 * LANES, width), bf16),
            jax.ShapeDtypeStruct((LANES, width), bf16),
            jax.ShapeDtypeStruct((LANES, width), bf16),
            jax.ShapeDtypeStruct((RANKS // 2, LANES), bf16),
        ),
        in_specs=[vmem] * len(sent),
        out_specs=(hbm, hbm, hbm, vmem),
        scratch_shapes=[
            pltpu.VMEM((CHUNKS, width, LANES), bf16),
            pltpu.VMEM((RANKS, 8, LANES), jnp.float32),
            pltpu.VMEM((CHUNKS, LANES, width), bf16),
            pltpu.SemaphoreType.DMA((CHUNKS,)),
        ],
        compiler_params=pltpu.CompilerParams(vmem_limit_bytes=16 * 2**20),
        name="place",
    )(*(pltpu.with_memory_space_constraint(a, pltpu.VMEM) for a in sent))
    return query, key, value, norm.reshape(width)


def solution(mesh):
    split = Mesh(
        mesh.devices.reshape(RING_0, RING_1, mesh.shape["tp"], mesh.shape["unit"]),
        ("rows_0", "rows_1", "tp", "unit"),
    )
    return jax.shard_map(
        shards,
        mesh=split,
        in_specs=(
            P(UNIT_ROWS, "tp"),
            P(UNIT_ROWS, None),
            P("unit", "tp"),
            P(UNIT_ROWS, "tp"),
            P(UNIT_ROWS, None),
            P("unit", "tp"),
            P(UNIT_ROWS, "tp"),
            P(UNIT_ROWS, None),
            P("unit", "tp"),
            P(UNIT_ROWS_TP),
            P(UNIT_ROWS_TP),
        ),
        out_specs=(
            P(("unit", "tp"), None),
            P(("unit", "tp"), None),
            P(("unit", "tp"), None),
            P("unit"),
        ),
        check_vma=False,
    )
```

profile of v0, /device:TPU:8, one launch (start us, length us, event | category | flops | bytes accessed | tf_op | source)
XLA Modules:
  0.0 61.4 jit_solution(3704156186501787050)
XLA Ops:
  0.7 0.7 %add_convert_fusion = bf16[16]{0:T(256)(128)(2,1)S(1)} fusion(f32[16]{0:T(128)} %param.20, f32[16]{0:T(128)} %param.21), kind=kLoop, calls=%fused_computation.24 | loop fusion | flops 32 | bytes 160 | tf_op jit(solution)/shard_map/convert_element_type | solution.py:111
  1.5 2.2 %collective-permute-start.2 = (bf16[8,128]{1,0:T(8,128)(2,1)S(1)}, bf16[8,128]{1,0:T(8,128)(2,1)S(1)}, u32[]{:S(2)}, u32[]{:S(2)}) collective-permute-start(bf16[8,128]{1,0:T(8,128)(2,1)S(1)} %fusion.4.own), channel_id=1, source_target_pairs={{0,6},{2,0},{4,2},{6,4},{1,7},{3,1},{5,3},{7,5},{8,14},{10,8},{12,... | collective-permute-start | bytes 6152 | tf_op jit(solution)/shard_map/ppermute | solution.py:114
  3.7 0.9 %collective-permute-start.1 = (bf16[8,128]{1,0:T(8,128)(2,1)S(1)}, bf16[8,128]{1,0:T(8,128)(2,1)S(1)}, u32[]{:S(2)}, u32[]{:S(2)}) collective-permute-start(bf16[8,128]{1,0:T(8,128)(2,1)S(1)} %fusion.4.own), channel_id=1, source_target_pairs={{0,4},{2,6},{4,0},{6,2},{1,5},{3,7},{5,1},{7,3},{8,12},{10,14},{12... | collective-permute-start | bytes 6152 | tf_op jit(solution)/shard_map/ppermute | solution.py:114
  4.6 1.9 %collective-permute-start = (bf16[8,128]{1,0:T(8,128)(2,1)S(1)}, bf16[8,128]{1,0:T(8,128)(2,1)S(1)}, u32[]{:S(2)}, u32[]{:S(2)}) collective-permute-start(bf16[8,128]{1,0:T(8,128)(2,1)S(1)} %fusion.4.own), channel_id=1, source_target_pairs={{0,2},{2,4},{4,6},{6,0},{1,3},{3,5},{5,7},{7,1},{8,10},{10,12},{12... | collective-permute-start | bytes 6152 | tf_op jit(solution)/shard_map/ppermute | solution.py:114
  6.5 1.1 %merge.1._ = bf16[392,128]{1,0:T(8,128)(2,1)S(1)} custom-call(bf16[64,512]{1,0:T(8,128)(2,1)} %tq.1, bf16[64,64]{1,0:T(8,128)(2,1)} %lq.1, bf16[64,512]{1,0:T(8,128)(2,1)} %hq.1, bf16[64,128]{1,0:T(8,128)(2,1)} %tk.1, bf16[64,64]{1,0:T(8,128)(2,1)} %lk.1, bf16[64,128]{1,0:T(8,128)(2,1)} %hk.1, bf16[64,128]{1,0:T(8,128)(2,1)} %tv.1, bf16[64,64]{1,0:T(8,128)(2,1)} %lv.1, ...), custom_call_target="tpu_custom_call" | custom-call | tf_op jit(solution)/shard_map/merge/pallas_call | solution.py:115
  7.6 1.2 %collective-permute-done.1.second = bf16[8,128]{1,0:T(8,128)(2,1)S(1)} collective-permute-done((bf16[8,128]{1,0:T(8,128)(2,1)S(1)}, bf16[8,128]{1,0:T(8,128)(2,1)S(1)}, u32[]{:S(2)}, u32[]{:S(2)}) %collective-permute-start.1) | collective-permute-done | bytes 2080 | tf_op jit(solution)/shard_map/ppermute | solution.py:114
  8.8 2.4 %collective-permute-start.4 = (bf16[392,128]{1,0:T(8,128)(2,1)S(1)}, bf16[392,128]{1,0:T(8,128)(2,1)S(1)}, u32[]{:S(2)}, u32[]{:S(2)}) collective-permute-start(bf16[392,128]{1,0:T(8,128)(2,1)S(1)} %gain.1.refs_0_), channel_id=1, source_target_pairs={{16,0},{24,8},{0,16},{8,24},{48,32},{56,40},{32,48},{40,56},{80,64... | collective-permute-start | bytes 301064 | tf_op jit(solution)/shard_map/ppermute | solution.py:49
  11.2 3.3 %collective-permute-start.6 = (bf16[392,128]{1,0:T(8,128)(2,1)S(1)}, bf16[392,128]{1,0:T(8,128)(2,1)S(1)}, u32[]{:S(2)}, u32[]{:S(2)}) collective-permute-start(bf16[392,128]{1,0:T(8,128)(2,1)S(1)} %gain.1.refs_0_), channel_id=1, source_target_pairs={{192,0},{200,8},{208,16},{216,24},{224,32},{232,40},{240,48},{248,... | collective-permute-start | bytes 301064 | tf_op jit(solution)/shard_map/ppermute | solution.py:49
  14.5 3.0 %collective-permute-start.5 = (bf16[392,128]{1,0:T(8,128)(2,1)S(1)}, bf16[392,128]{1,0:T(8,128)(2,1)S(1)}, u32[]{:S(2)}, u32[]{:S(2)}) collective-permute-start(bf16[392,128]{1,0:T(8,128)(2,1)S(1)} %gain.1.refs_0_), channel_id=1, source_target_pairs={{64,0},{72,8},{80,16},{88,24},{96,32},{104,40},{112,48},{120,56},{... | collective-permute-start | bytes 301064 | tf_op jit(solution)/shard_map/ppermute | solution.py:49
  17.5 5.0 %collective-permute-start.3 = (bf16[392,128]{1,0:T(8,128)(2,1)S(1)}, bf16[392,128]{1,0:T(8,128)(2,1)S(1)}, u32[]{:S(2)}, u32[]{:S(2)}) collective-permute-start(bf16[392,128]{1,0:T(8,128)(2,1)S(1)} %gain.1.refs_0_), channel_id=1, source_target_pairs={{128,0},{136,8},{144,16},{152,24},{160,32},{168,40},{176,48},{184,... | collective-permute-start | bytes 301064 | tf_op jit(solution)/shard_map/ppermute | solution.py:49
  22.5 1.1 %collective-permute-start.7 = (bf16[784,128]{1,0:T(8,128)(2,1)S(1)}, bf16[784,128]{1,0:T(8,128)(2,1)S(1)}, u32[]{:S(2)}, u32[]{:S(2)}) collective-permute-start(bf16[784,128]{1,0:T(8,128)(2,1)S(1)} %pad_maximum_fusion.4), channel_id=1, source_target_pairs={{224,0},{232,8},{240,16},{248,24},{0,32},{8,40},{16,48},{24,56},{3... | collective-permute-start | bytes 602120 | tf_op jit(solution)/shard_map/ppermute | solution.py:49
  23.6 4.6 %collective-permute-done.3.refs_1_ = bf16[392,128]{1,0:T(8,128)(2,1)S(1)} collective-permute-done((bf16[392,128]{1,0:T(8,128)(2,1)S(1)}, bf16[392,128]{1,0:T(8,128)(2,1)S(1)}, u32[]{:S(2)}, u32[]{:S(2)}) %collective-permute-start.3) | collective-permute-done | bytes 100384 | tf_op jit(solution)/shard_map/ppermute | solution.py:49
  28.3 1.2 %collective-permute-start.12 = (bf16[1176,128]{1,0:T(8,128)(2,1)S(1)}, bf16[1176,128]{1,0:T(8,128)(2,1)S(1)}, u32[]{:S(2)}, u32[]{:S(2)}) collective-permute-start(bf16[1176,128]{1,0:T(8,128)(2,1)S(1)} %get-tuple-element.17), channel_id=1, source_target_pairs={{8,0},{16,8},{24,16},{0,24},{40,32},{48,40},{56,48},{32,56},{72,64... | collective-permute-start | bytes 903176 | tf_op jit(solution)/shard_map/ppermute | solution.py:49
  29.5 1.6 %collective-permute-start.9 = (bf16[1176,128]{1,0:T(8,128)(2,1)S(1)}, bf16[1176,128]{1,0:T(8,128)(2,1)S(1)}, u32[]{:S(2)}, u32[]{:S(2)}) collective-permute-start(bf16[1176,128]{1,0:T(8,128)(2,1)S(1)} %get-tuple-element.18), channel_id=1, source_target_pairs={{32,0},{40,8},{48,16},{56,24},{64,32},{72,40},{80,48},{88,56},{96,... | collective-permute-start | bytes 903176 | tf_op jit(solution)/shard_map/ppermute | solution.py:49
  31.2 1.9 %collective-permute-start.8 = (bf16[392,128]{1,0:T(8,128)(2,1)S(1)}, bf16[392,128]{1,0:T(8,128)(2,1)S(1)}, u32[]{:S(2)}, u32[]{:S(2)}) collective-permute-start(bf16[392,128]{1,0:T(8,128)(2,1)S(1)} %collective-permute-done.3.refs_1_), channel_id=1, source_target_pairs={{24,0},{0,8},{8,16},{16,24},{56,32},{32,40},{40,48},{48,56},{88,64... | collective-permute-start | bytes 301064 | tf_op jit(solution)/shard_map/ppermute | solution.py:49
  33.2 3.9 %collective-permute-done.8.refs_6_ = bf16[392,128]{1,0:T(8,128)(2,1)S(1)} collective-permute-done((bf16[392,128]{1,0:T(8,128)(2,1)S(1)}, bf16[392,128]{1,0:T(8,128)(2,1)S(1)}, u32[]{:S(2)}, u32[]{:S(2)}) %collective-permute-start.8) | collective-permute-done | bytes 100384 | tf_op jit(solution)/shard_map/ppermute | solution.py:49
  37.1 2.2 %collective-permute-start.14 = (bf16[784,128]{1,0:T(8,128)(2,1)S(1)}, bf16[784,128]{1,0:T(8,128)(2,1)S(1)}, u32[]{:S(2)}, u32[]{:S(2)}) collective-permute-start(bf16[784,128]{1,0:T(8,128)(2,1)S(1)} %constant_dynamic-update-slice_fusion), channel_id=1, source_target_pairs={{32,0},{40,8},{48,16},{56,24},{64,32},{72,40},{80,48},{88,56},{96,... | collective-permute-start | bytes 602120 | tf_op jit(solution)/shard_map/ppermute | solution.py:49
  39.3 1.5 %collective-permute-start.11 = (bf16[784,128]{1,0:T(8,128)(2,1)S(1)}, bf16[784,128]{1,0:T(8,128)(2,1)S(1)}, u32[]{:S(2)}, u32[]{:S(2)}) collective-permute-start(bf16[784,128]{1,0:T(8,128)(2,1)S(1)} %constant_dynamic-update-slice_fusion), channel_id=1, source_target_pairs={{24,0},{0,8},{8,16},{16,24},{56,32},{32,40},{40,48},{48,56},{88,64... | collective-permute-start | bytes 602120 | tf_op jit(solution)/shard_map/ppermute | solution.py:49
  41.0 7.3 %collective-permute-done.11.refs_9_ = bf16[784,128]{1,0:T(8,128)(2,1)S(1)} collective-permute-done((bf16[784,128]{1,0:T(8,128)(2,1)S(1)}, bf16[784,128]{1,0:T(8,128)(2,1)S(1)}, u32[]{:S(2)}, u32[]{:S(2)}) %collective-permute-start.11) | collective-permute-done | bytes 200736 | tf_op jit(solution)/shard_map/ppermute | solution.py:49
  48.3 0.4 collective-permute-start.15
  49.1 2.9 %collective-permute-start.17 = (bf16[784,128]{1,0:T(8,128)(2,1)S(1)}, bf16[784,128]{1,0:T(8,128)(2,1)S(1)}, u32[]{:S(2)}, u32[]{:S(2)}) collective-permute-start(bf16[784,128]{1,0:T(8,128)(2,1)S(1)} %pad_maximum_fusion.6), channel_id=1, source_target_pairs={{8,0},{16,8},{24,16},{0,24},{40,32},{48,40},{56,48},{32,56},{72,64... | collective-permute-start | bytes 602120 | tf_op jit(solution)/shard_map/ppermute | solution.py:49
  52.0 3.2 %collective-permute-start.18 = (bf16[784,128]{1,0:T(8,128)(2,1)S(1)}, bf16[784,128]{1,0:T(8,128)(2,1)S(1)}, u32[]{:S(2)}, u32[]{:S(2)}) collective-permute-start(bf16[784,128]{1,0:T(8,128)(2,1)S(1)} %pad_maximum_fusion.7), channel_id=1, source_target_pairs={{32,0},{40,8},{48,16},{56,24},{64,32},{72,40},{80,48},{88,56},{96,... | collective-permute-start | bytes 602120 | tf_op jit(solution)/shard_map/ppermute | solution.py:49
  55.2 3.2 %collective-permute-done.18.refs_16_ = bf16[784,128]{1,0:T(8,128)(2,1)S(1)} collective-permute-done((bf16[784,128]{1,0:T(8,128)(2,1)S(1)}, bf16[784,128]{1,0:T(8,128)(2,1)S(1)}, u32[]{:S(2)}, u32[]{:S(2)}) %collective-permute-start.18) | collective-permute-done | bytes 200736 | tf_op jit(solution)/shard_map/ppermute | solution.py:49
  58.5 2.7 %place.1 = (bf16[512,2048]{1,0:T(8,128)(2,1)}, bf16[128,2048]{1,0:T(8,128)(2,1)}, bf16[128,2048]{1,0:T(8,128)(2,1)}, bf16[16,128]{1,0:T(8,128)(2,1)}) custom-call(bf16[392,128]{1,0:T(8,128)(2,1)S(1)} %gain.1.refs_0_, bf16[392,128]{1,0:T(8,128)(2,1)S(1)} %collective-permute-done.3.refs_1_, bf16[392,128]{1,0:T(8,128)(2,1)S(1)} %collective-permute-done.4.refs_2_, ...), custom_call_target="tpu_custom_call" | custom-call | tf_op jit(solution)/shard_map/place/pallas_call | solution.py:143
  (35 shorter events, 0.8 us)
Async XLA Ops:
  1.5 6.1 %collective-permute-start.2 = (bf16[8,128]{1,0:T(8,128)(2,1)S(1)}, bf16[8,128]{1,0:T(8,128)(2,1)S(1)}, u32[]{:S(2)}, u32[]{:S(2)}) collective-permute-start(bf16[8,128]{1,0:T(8,128)(2,1)S(1)} %fusion.4.own), channel_id=1, source_target_pairs={{0,6},{2,0},{4,2},{6,4},{1,7},{3,1},{5,3},{7,5},{8,14},{10,8},{12,... | collective-permute-start | bytes 6152 | tf_op jit(solution)/shard_map/ppermute | solution.py:114
  3.7 5.1 %collective-permute-start.1 = (bf16[8,128]{1,0:T(8,128)(2,1)S(1)}, bf16[8,128]{1,0:T(8,128)(2,1)S(1)}, u32[]{:S(2)}, u32[]{:S(2)}) collective-permute-start(bf16[8,128]{1,0:T(8,128)(2,1)S(1)} %fusion.4.own), channel_id=1, source_target_pairs={{0,4},{2,6},{4,0},{6,2},{1,5},{3,7},{5,1},{7,3},{8,12},{10,14},{12... | collective-permute-start | bytes 6152 | tf_op jit(solution)/shard_map/ppermute | solution.py:114
  4.6 4.2 %collective-permute-start = (bf16[8,128]{1,0:T(8,128)(2,1)S(1)}, bf16[8,128]{1,0:T(8,128)(2,1)S(1)}, u32[]{:S(2)}, u32[]{:S(2)}) collective-permute-start(bf16[8,128]{1,0:T(8,128)(2,1)S(1)} %fusion.4.own), channel_id=1, source_target_pairs={{0,2},{2,4},{4,6},{6,0},{1,3},{3,5},{5,7},{7,1},{8,10},{10,12},{12... | collective-permute-start | bytes 6152 | tf_op jit(solution)/shard_map/ppermute | solution.py:114
  8.8 13.7 %collective-permute-start.4 = (bf16[392,128]{1,0:T(8,128)(2,1)S(1)}, bf16[392,128]{1,0:T(8,128)(2,1)S(1)}, u32[]{:S(2)}, u32[]{:S(2)}) collective-permute-start(bf16[392,128]{1,0:T(8,128)(2,1)S(1)} %gain.1.refs_0_), channel_id=1, source_target_pairs={{16,0},{24,8},{0,16},{8,24},{48,32},{56,40},{32,48},{40,56},{80,64... | collective-permute-start | bytes 301064 | tf_op jit(solution)/shard_map/ppermute | solution.py:49
  11.2 12.4 %collective-permute-start.6 = (bf16[392,128]{1,0:T(8,128)(2,1)S(1)}, bf16[392,128]{1,0:T(8,128)(2,1)S(1)}, u32[]{:S(2)}, u32[]{:S(2)}) collective-permute-start(bf16[392,128]{1,0:T(8,128)(2,1)S(1)} %gain.1.refs_0_), channel_id=1, source_target_pairs={{192,0},{200,8},{208,16},{216,24},{224,32},{232,40},{240,48},{248,... | collective-permute-start | bytes 301064 | tf_op jit(solution)/shard_map/ppermute | solution.py:49
  14.5 9.2 %collective-permute-start.5 = (bf16[392,128]{1,0:T(8,128)(2,1)S(1)}, bf16[392,128]{1,0:T(8,128)(2,1)S(1)}, u32[]{:S(2)}, u32[]{:S(2)}) collective-permute-start(bf16[392,128]{1,0:T(8,128)(2,1)S(1)} %gain.1.refs_0_), channel_id=1, source_target_pairs={{64,0},{72,8},{80,16},{88,24},{96,32},{104,40},{112,48},{120,56},{... | collective-permute-start | bytes 301064 | tf_op jit(solution)/shard_map/ppermute | solution.py:49
  17.5 10.8 %collective-permute-start.3 = (bf16[392,128]{1,0:T(8,128)(2,1)S(1)}, bf16[392,128]{1,0:T(8,128)(2,1)S(1)}, u32[]{:S(2)}, u32[]{:S(2)}) collective-permute-start(bf16[392,128]{1,0:T(8,128)(2,1)S(1)} %gain.1.refs_0_), channel_id=1, source_target_pairs={{128,0},{136,8},{144,16},{152,24},{160,32},{168,40},{176,48},{184,... | collective-permute-start | bytes 301064 | tf_op jit(solution)/shard_map/ppermute | solution.py:49
  22.5 18.3 %collective-permute-start.7 = (bf16[784,128]{1,0:T(8,128)(2,1)S(1)}, bf16[784,128]{1,0:T(8,128)(2,1)S(1)}, u32[]{:S(2)}, u32[]{:S(2)}) collective-permute-start(bf16[784,128]{1,0:T(8,128)(2,1)S(1)} %pad_maximum_fusion.4), channel_id=1, source_target_pairs={{224,0},{232,8},{240,16},{248,24},{0,32},{8,40},{16,48},{24,56},{3... | collective-permute-start | bytes 602120 | tf_op jit(solution)/shard_map/ppermute | solution.py:49
  28.3 26.9 %collective-permute-start.12 = (bf16[1176,128]{1,0:T(8,128)(2,1)S(1)}, bf16[1176,128]{1,0:T(8,128)(2,1)S(1)}, u32[]{:S(2)}, u32[]{:S(2)}) collective-permute-start(bf16[1176,128]{1,0:T(8,128)(2,1)S(1)} %get-tuple-element.17), channel_id=1, source_target_pairs={{8,0},{16,8},{24,16},{0,24},{40,32},{48,40},{56,48},{32,56},{72,64... | collective-permute-start | bytes 903176 | tf_op jit(solution)/shard_map/ppermute | solution.py:49
  29.5 19.2 %collective-permute-start.9 = (bf16[1176,128]{1,0:T(8,128)(2,1)S(1)}, bf16[1176,128]{1,0:T(8,128)(2,1)S(1)}, u32[]{:S(2)}, u32[]{:S(2)}) collective-permute-start(bf16[1176,128]{1,0:T(8,128)(2,1)S(1)} %get-tuple-element.18), channel_id=1, source_target_pairs={{32,0},{40,8},{48,16},{56,24},{64,32},{72,40},{80,48},{88,56},{96,... | collective-permute-start | bytes 903176 | tf_op jit(solution)/shard_map/ppermute | solution.py:49
  31.1 8.2 %collective-permute-start.10 = (bf16[392,128]{1,0:T(8,128)(2,1)S(1)}, bf16[392,128]{1,0:T(8,128)(2,1)S(1)}, u32[]{:S(2)}, u32[]{:S(2)}) collective-permute-start(bf16[392,128]{1,0:T(8,128)(2,1)S(1)} %collective-permute-done.3.refs_1_), channel_id=1, source_target_pairs={{8,0},{16,8},{24,16},{0,24},{40,32},{48,40},{56,48},{32,56},{72,64... | collective-permute-start | bytes 301064 | tf_op jit(solution)/shard_map/ppermute | solution.py:49
  31.2 5.8 %collective-permute-start.8 = (bf16[392,128]{1,0:T(8,128)(2,1)S(1)}, bf16[392,128]{1,0:T(8,128)(2,1)S(1)}, u32[]{:S(2)}, u32[]{:S(2)}) collective-permute-start(bf16[392,128]{1,0:T(8,128)(2,1)S(1)} %collective-permute-done.3.refs_1_), channel_id=1, source_target_pairs={{24,0},{0,8},{8,16},{16,24},{56,32},{32,40},{40,48},{48,56},{88,64... | collective-permute-start | bytes 301064 | tf_op jit(solution)/shard_map/ppermute | solution.py:49
  37.1 12.0 %collective-permute-start.14 = (bf16[784,128]{1,0:T(8,128)(2,1)S(1)}, bf16[784,128]{1,0:T(8,128)(2,1)S(1)}, u32[]{:S(2)}, u32[]{:S(2)}) collective-permute-start(bf16[784,128]{1,0:T(8,128)(2,1)S(1)} %constant_dynamic-update-slice_fusion), channel_id=1, source_target_pairs={{32,0},{40,8},{48,16},{56,24},{64,32},{72,40},{80,48},{88,56},{96,... | collective-permute-start | bytes 602120 | tf_op jit(solution)/shard_map/ppermute | solution.py:49
  39.3 9.0 %collective-permute-start.11 = (bf16[784,128]{1,0:T(8,128)(2,1)S(1)}, bf16[784,128]{1,0:T(8,128)(2,1)S(1)}, u32[]{:S(2)}, u32[]{:S(2)}) collective-permute-start(bf16[784,128]{1,0:T(8,128)(2,1)S(1)} %constant_dynamic-update-slice_fusion), channel_id=1, source_target_pairs={{24,0},{0,8},{8,16},{16,24},{56,32},{32,40},{40,48},{48,56},{88,64... | collective-permute-start | bytes 602120 | tf_op jit(solution)/shard_map/ppermute | solution.py:49
  40.8 11.2 %collective-permute-start.13 = (bf16[784,128]{1,0:T(8,128)(2,1)S(1)}, bf16[784,128]{1,0:T(8,128)(2,1)S(1)}, u32[]{:S(2)}, u32[]{:S(2)}) collective-permute-start(bf16[784,128]{1,0:T(8,128)(2,1)S(1)} %pad_maximum_fusion.5), channel_id=1, source_target_pairs={{224,0},{232,8},{240,16},{248,24},{0,32},{8,40},{16,48},{24,56},{3... | collective-permute-start | bytes 602120 | tf_op jit(solution)/shard_map/ppermute | solution.py:49
  48.3 10.2 %collective-permute-start.15 = (bf16[1568,128]{1,0:T(8,128)(2,1)S(1)}, bf16[1568,128]{1,0:T(8,128)(2,1)S(1)}, u32[]{:S(2)}, u32[]{:S(2)}) collective-permute-start(bf16[1568,128]{1,0:T(8,128)(2,1)S(1)} %pad_maximum_fusion), channel_id=1, source_target_pairs={{24,0},{0,8},{8,16},{16,24},{56,32},{32,40},{40,48},{48,56},{88,64... | collective-permute-start | bytes 1204232 | tf_op jit(solution)/shard_map/ppermute | solution.py:49
  48.7 9.7 %collective-permute-start.16 = (bf16[1176,128]{1,0:T(8,128)(2,1)S(1)}, bf16[1176,128]{1,0:T(8,128)(2,1)S(1)}, u32[]{:S(2)}, u32[]{:S(2)}) collective-permute-start(bf16[1176,128]{1,0:T(8,128)(2,1)S(1)} %pad_maximum_fusion.3), channel_id=1, source_target_pairs={{224,0},{232,8},{240,16},{248,24},{0,32},{8,40},{16,48},{24,56},{3... | collective-permute-start | bytes 903176 | tf_op jit(solution)/shard_map/ppermute | solution.py:49
  49.1 6.2 %collective-permute-start.17 = (bf16[784,128]{1,0:T(8,128)(2,1)S(1)}, bf16[784,128]{1,0:T(8,128)(2,1)S(1)}, u32[]{:S(2)}, u32[]{:S(2)}) collective-permute-start(bf16[784,128]{1,0:T(8,128)(2,1)S(1)} %pad_maximum_fusion.6), channel_id=1, source_target_pairs={{8,0},{16,8},{24,16},{0,24},{40,32},{48,40},{56,48},{32,56},{72,64... | collective-permute-start | bytes 602120 | tf_op jit(solution)/shard_map/ppermute | solution.py:49
  52.0 6.4 %collective-permute-start.18 = (bf16[784,128]{1,0:T(8,128)(2,1)S(1)}, bf16[784,128]{1,0:T(8,128)(2,1)S(1)}, u32[]{:S(2)}, u32[]{:S(2)}) collective-permute-start(bf16[784,128]{1,0:T(8,128)(2,1)S(1)} %pad_maximum_fusion.7), channel_id=1, source_target_pairs={{32,0},{40,8},{48,16},{56,24},{64,32},{72,40},{80,48},{88,56},{96,... | collective-permute-start | bytes 602120 | tf_op jit(solution)/shard_map/ppermute | solution.py:49
where the time goes:
time: 61.9 us; the launch traced here: 61.4 us
  starting transfers between devices  35.2 us (57%)
  waiting for transfers between devices  20.3 us (33%)
  Pallas kernels  3.84 us (6%)
  between operations  0.96 us (2%)
  other arithmetic  0.87 us (1%)
    ppermute x16, starting transfers between devices, from_offset(): return lax.ppermute(array, ROWS, pairs)  30.2 us
    ppermute x16, waiting for transfers between devices, from_offset(): return lax.ppermute(array, ROWS, pairs)  19.1 us
    ppermute x3, starting transfers between devices, shards(): lax.ppermute(gain, 'tp', [(i, (i + s) % TP) for i in range(TP)])  5 us
    pallas_call x1, Pallas kernels, shards(): pl.pallas_call(lambda *refs: place_kernel(pieces, *refs), out_shape=(jax....  2.73 us
  transfers between devices with their start and end apart: 19, of which 5 were waited for; matrix products, arithmetic and copies ran while one was open for 0% of the time, Pallas kernels for 2%

commit v1 on v0

--- a/solution.py
+++ b/solution.py
@@ -22,21 +22,17 @@
 
 STEPS = (
     ((4, 0), ((0, 0),)),
-    ((0, 2), ((0, 0),)),
-    ((2, 0), ((0, 0),)),
-    ((6, 0), ((0, 0),)),
-    ((-1, 0), ((0, 0), (0, 2))),
-    ((0, -1), ((4, 0),)),
-    ((1, 0), ((0, 0), (0, 2), (4, 0))),
-    ((0, 1), ((4, 0),)),
-    ((0, -1), ((2, 0), (4, 3))),
-    ((0, 1), ((0, 0), (2, 0), (6, 0))),
-    ((-1, 0), ((4, 1), (4, 3))),
-    ((1, 0), ((2, 0), (4, 3))),
-    ((0, -1), ((0, 0), (6, 0), (7, 2), (7, 0))),
-    ((-1, 0), ((2, 3), (4, 2), (7, 2))),
-    ((0, 1), ((1, 0), (5, 0))),
-    ((1, 0), ((1, 2), (4, 2))),
+    ((7, 0), ((0, 0),)),
+    ((2, 2), ((0, 0),)),
+    ((6, 2), ((0, 0),)),
+    ((1, 0), ((0, 0), (4, 0))),
+    ((0, 1), ((0, 0), (4, 0))),
+    ((0, -1), ((2, 2), (4, 0))),
+    ((-1, 0), ((2, 2), (4, 0), (7, 0))),
+    ((0, -1), ((0, 0), (1, 0), (5, 0), (6, 2), (7, 0))),
+    ((0, 1), ((0, 1), (2, 2), (4, 1), (6, 2), (7, 0))),
+    ((1, 0), ((1, 0), (2, 2), (4, 1), (6, 2))),
+    ((-1, 0), ((2, 1), (4, 1), (4, 3), (6, 2))),
 )
 
 
@@ -64,6 +60,27 @@
 
 def gain_kernel(_, own, first, second, third, out):
     out[WEIGHT_ROWS:, :] = own[...] + first[...] + second[...] + third[...]
+
+
+def pack(sent, parts):
+    if len(parts) == 1 and sent[parts[0][0]].shape[0] == SENT_ROWS:
+        return sent[parts[0][0]]
+    used = sorted({at for at, _ in parts})
+
+    def kernel(*refs):
+        for number, (at, row) in enumerate(parts):
+            to = number * SENT_ROWS
+            refs[-1][to : to + SENT_ROWS, :] = refs[used.index(at)][row : row + SENT_ROWS, :]
+
+    vmem = pl.BlockSpec(memory_space=pltpu.VMEM)
+    return pl.pallas_call(
+        kernel,
+        out_shape=pltpu.VMEM((len(parts) * SENT_ROWS, LANES), jnp.bfloat16),
+        in_specs=[vmem] * len(used),
+        out_specs=vmem,
+        compiler_params=pltpu.CompilerParams(vmem_limit_bytes=2**20),
+        name="pack",
+    )(*(pltpu.with_memory_space_constraint(sent[at], pltpu.VMEM) for at in used))
 
 
 def place_kernel(pieces, *refs):
@@ -130,8 +147,7 @@
 
     sent, held = [block], {(0, 0): (0, 0)}
     for offset, passed in STEPS:
-        parts = [sent[at][row : row + SENT_ROWS] for at, row in (held[p] for p in passed)]
-        arrived = from_offset(parts[0] if len(parts) == 1 else jnp.concatenate(parts, axis=0), *offset)
+        arrived = from_offset(pack(sent, [held[p] for p in passed]), *offset)
         for place, (dz, dx) in enumerate(passed):
             held[(offset[0] + dz) % RING_0, (offset[1] + dx) % RING_1] = (len(sent), place * SENT_ROWS)
         sent.append(arrived)

time: 61.9 us -> 55.9 us (0.903)
  starting transfers between devices: 35.2 us -> 29 us
  waiting for transfers between devices: 20.3 us -> 21.2 us
    ppermute x16 -> x12, starting transfers between devices: 30.2 us -> 24 us  [from_offset(): return lax.ppermute(array, ROWS, pairs)]
    ppermute x16 -> x12, waiting for transfers between devices: 19.1 us -> 20 us  [from_offset(): return lax.ppermute(array, ROWS, pairs)]
  transfers between devices with their start and end apart: 19 -> 15, of which waited for: 5 -> 4; matrix products, arithmetic and copies ran while one was open for 0% -> 0% of each run, Pallas kernels for 2% -> 2%
where the time goes in v1:
time: 55.9 us; the launch traced here: 55.8 us
  starting transfers between devices  29 us (52%)
  waiting for transfers between devices  21.2 us (38%)
  Pallas kernels  4.02 us (7%)
  between operations  0.75 us (1%)
  other arithmetic  0.71 us (1%)
    ppermute x12, starting transfers between devices, from_offset(): return lax.ppermute(array, ROWS, pairs)  24 us
    ppermute x12, waiting for transfers between devices, from_offset(): return lax.ppermute(array, ROWS, pairs)  20 us
    ppermute x3, starting transfers between devices, shards(): lax.ppermute(gain, 'tp', [(i, (i + s) % TP) for i in range(TP)])  5 us
    pallas_call x1, Pallas kernels, shards(): pl.pallas_call(lambda *refs: place_kernel(pieces, *refs), out_shape=(jax....  2.74 us
    ppermute x3, waiting for transfers between devices, shards(): lax.ppermute(gain, 'tp', [(i, (i + s) % TP) for i in range(TP)])  1.21 us
  transfers between devices with their start and end apart: 15, of which 4 were waited for; matrix products, arithmetic and copies ran while one was open for 0% of the time, Pallas kernels for 2%

profile of v1, /device:TPU:8, one launch (start us, length us, event | category | flops | bytes accessed | tf_op | source)
XLA Modules:
  0.0 55.8 jit_solution(16219455454250306494)
XLA Ops:
  0.7 0.7 %add_convert_fusion = bf16[16]{0:T(256)(128)(2,1)S(1)} fusion(f32[16]{0:T(128)} %param.20, f32[16]{0:T(128)} %param.21), kind=kLoop, calls=%fused_computation.12 | loop fusion | flops 32 | bytes 160 | tf_op jit(solution)/shard_map/convert_element_type | solution.py:128
  1.3 0.1 broadcast_in_dim.14
  1.5 2.2 %collective-permute-start.2 = (bf16[8,128]{1,0:T(8,128)(2,1)S(1)}, bf16[8,128]{1,0:T(8,128)(2,1)S(1)}, u32[]{:S(2)}, u32[]{:S(2)}) collective-permute-start(bf16[8,128]{1,0:T(8,128)(2,1)S(1)} %fusion.2.own), channel_id=1, source_target_pairs={{0,6},{2,0},{4,2},{6,4},{1,7},{3,1},{5,3},{7,5},{8,14},{10,8},{12,... | collective-permute-start | bytes 6152 | tf_op jit(solution)/shard_map/ppermute | solution.py:131
  3.7 0.9 %collective-permute-start.1 = (bf16[8,128]{1,0:T(8,128)(2,1)S(1)}, bf16[8,128]{1,0:T(8,128)(2,1)S(1)}, u32[]{:S(2)}, u32[]{:S(2)}) collective-permute-start(bf16[8,128]{1,0:T(8,128)(2,1)S(1)} %fusion.2.own), channel_id=1, source_target_pairs={{0,4},{2,6},{4,0},{6,2},{1,5},{3,7},{5,1},{7,3},{8,12},{10,14},{12... | collective-permute-start | bytes 6152 | tf_op jit(solution)/shard_map/ppermute | solution.py:131
  4.6 1.9 %collective-permute-start = (bf16[8,128]{1,0:T(8,128)(2,1)S(1)}, bf16[8,128]{1,0:T(8,128)(2,1)S(1)}, u32[]{:S(2)}, u32[]{:S(2)}) collective-permute-start(bf16[8,128]{1,0:T(8,128)(2,1)S(1)} %fusion.2.own), channel_id=1, source_target_pairs={{0,2},{2,4},{4,6},{6,0},{1,3},{3,5},{5,7},{7,1},{8,10},{10,12},{12... | collective-permute-start | bytes 6152 | tf_op jit(solution)/shard_map/ppermute | solution.py:131
  6.5 1.1 %merge.1._ = bf16[392,128]{1,0:T(8,128)(2,1)S(1)} custom-call(bf16[64,512]{1,0:T(8,128)(2,1)} %tq.1, bf16[64,64]{1,0:T(8,128)(2,1)} %lq.1, bf16[64,512]{1,0:T(8,128)(2,1)} %hq.1, bf16[64,128]{1,0:T(8,128)(2,1)} %tk.1, bf16[64,64]{1,0:T(8,128)(2,1)} %lk.1, bf16[64,128]{1,0:T(8,128)(2,1)} %hk.1, bf16[64,128]{1,0:T(8,128)(2,1)} %tv.1, bf16[64,64]{1,0:T(8,128)(2,1)} %lv.1, ...), custom_call_target="tpu_custom_call" | custom-call | tf_op jit(solution)/shard_map/merge/pallas_call | solution.py:132
  7.6 1.2 %collective-permute-done.1.second = bf16[8,128]{1,0:T(8,128)(2,1)S(1)} collective-permute-done((bf16[8,128]{1,0:T(8,128)(2,1)S(1)}, bf16[8,128]{1,0:T(8,128)(2,1)S(1)}, u32[]{:S(2)}, u32[]{:S(2)}) %collective-permute-start.1) | collective-permute-done | bytes 2080 | tf_op jit(solution)/shard_map/ppermute | solution.py:131
  8.8 0.0 collective-permute-done.first
  8.8 6.6 %collective-permute-start.3 = (bf16[392,128]{1,0:T(8,128)(2,1)S(1)}, bf16[392,128]{1,0:T(8,128)(2,1)S(1)}, u32[]{:S(2)}, u32[]{:S(2)}) collective-permute-start(bf16[392,128]{1,0:T(8,128)(2,1)S(1)} %gain.1.refs_0_), channel_id=1, source_target_pairs={{128,0},{136,8},{144,16},{152,24},{160,32},{168,40},{176,48},{184,... | collective-permute-start | bytes 301064 | tf_op jit(solution)/shard_map/ppermute | solution.py:45
  15.4 2.1 %collective-permute-start.5 = (bf16[392,128]{1,0:T(8,128)(2,1)S(1)}, bf16[392,128]{1,0:T(8,128)(2,1)S(1)}, u32[]{:S(2)}, u32[]{:S(2)}) collective-permute-start(bf16[392,128]{1,0:T(8,128)(2,1)S(1)} %gain.1.refs_0_), channel_id=1, source_target_pairs={{80,0},{88,8},{64,16},{72,24},{112,32},{120,40},{96,48},{104,56},{... | collective-permute-start | bytes 301064 | tf_op jit(solution)/shard_map/ppermute | solution.py:45
  17.5 0.7 %collective-permute-done.3.refs_1_.refs_0_ = bf16[392,128]{1,0:T(8,128)(2,1)S(1)} collective-permute-done((bf16[392,128]{1,0:T(8,128)(2,1)S(1)}, bf16[392,128]{1,0:T(8,128)(2,1)S(1)}, u32[]{:S(2)}, u32[]{:S(2)}) %collective-permute-start.3) | collective-permute-done | bytes 100384 | tf_op jit(solution)/shard_map/ppermute | solution.py:45
  18.2 2.8 %collective-permute-start.8 = (bf16[784,128]{1,0:T(8,128)(2,1)S(1)}, bf16[784,128]{1,0:T(8,128)(2,1)S(1)}, u32[]{:S(2)}, u32[]{:S(2)}) collective-permute-start(bf16[784,128]{1,0:T(8,128)(2,1)S(1)} %pack.7), channel_id=1, source_target_pairs={{8,0},{16,8},{24,16},{0,24},{40,32},{48,40},{56,48},{32,56},{72,64... | collective-permute-start | bytes 602120 | tf_op jit(solution)/shard_map/ppermute | solution.py:45
  21.0 6.6 %collective-permute-start.7 = (bf16[784,128]{1,0:T(8,128)(2,1)S(1)}, bf16[784,128]{1,0:T(8,128)(2,1)S(1)}, u32[]{:S(2)}, u32[]{:S(2)}) collective-permute-start(bf16[784,128]{1,0:T(8,128)(2,1)S(1)} %pack.7), channel_id=1, source_target_pairs={{32,0},{40,8},{48,16},{56,24},{64,32},{72,40},{80,48},{88,56},{96,... | collective-permute-start | bytes 602120 | tf_op jit(solution)/shard_map/ppermute | solution.py:45
  27.6 0.0 collective-permute-start.6
  27.6 0.0 collective-permute-start.4
  27.7 0.3 collective-permute-start.9
  27.9 9.1 %collective-permute-done.6.refs_2_.refs_1_.refs_0_.refs_4_ = bf16[392,128]{1,0:T(8,128)(2,1)S(1)} collective-permute-done((bf16[392,128]{1,0:T(8,128)(2,1)S(1)}, bf16[392,128]{1,0:T(8,128)(2,1)S(1)}, u32[]{:S(2)}, u32[]{:S(2)}) %collective-permute-start.6) | collective-permute-done | bytes 100384 | tf_op jit(solution)/shard_map/ppermute | solution.py:45
  37.0 0.7 %collective-permute-start.12 = (bf16[1960,128]{1,0:T(8,128)(2,1)S(1)}, bf16[1960,128]{1,0:T(8,128)(2,1)S(1)}, u32[]{:S(2)}, u32[]{:S(2)}) collective-permute-start(bf16[1960,128]{1,0:T(8,128)(2,1)S(1)} %pack.11), channel_id=1, source_target_pairs={{8,0},{16,8},{24,16},{0,24},{40,32},{48,40},{56,48},{32,56},{72,64... | collective-permute-start | bytes 1505288 | tf_op jit(solution)/shard_map/ppermute | solution.py:45
  37.8 1.5 %collective-permute-start.11 = (bf16[1960,128]{1,0:T(8,128)(2,1)S(1)}, bf16[1960,128]{1,0:T(8,128)(2,1)S(1)}, u32[]{:S(2)}, u32[]{:S(2)}) collective-permute-start(bf16[1960,128]{1,0:T(8,128)(2,1)S(1)} %pack.10), channel_id=1, source_target_pairs={{24,0},{0,8},{8,16},{16,24},{56,32},{32,40},{40,48},{48,56},{88,64... | collective-permute-start | bytes 1505288 | tf_op jit(solution)/shard_map/ppermute | solution.py:45
  39.3 0.1 collective-permute-start.14
  39.4 3.3 %collective-permute-start.13 = (bf16[1568,128]{1,0:T(8,128)(2,1)S(1)}, bf16[1568,128]{1,0:T(8,128)(2,1)S(1)}, u32[]{:S(2)}, u32[]{:S(2)}) collective-permute-start(bf16[1568,128]{1,0:T(8,128)(2,1)S(1)} %pack.12), channel_id=1, source_target_pairs={{32,0},{40,8},{48,16},{56,24},{64,32},{72,40},{80,48},{88,56},{96,... | collective-permute-start | bytes 1204232 | tf_op jit(solution)/shard_map/ppermute | solution.py:45
  42.7 0.1 collective-permute-start.10
  42.8 10.2 %collective-permute-done.10.refs_8_ = bf16[1176,128]{1,0:T(8,128)(2,1)S(1)} collective-permute-done((bf16[1176,128]{1,0:T(8,128)(2,1)S(1)}, bf16[1176,128]{1,0:T(8,128)(2,1)S(1)}, u32[]{:S(2)}, u32[]{:S(2)}) %collective-permute-start.10) | collective-permute-done | bytes 301088 | tf_op jit(solution)/shard_map/ppermute | solution.py:45
  53.0 2.7 %place.1 = (bf16[512,2048]{1,0:T(8,128)(2,1)}, bf16[128,2048]{1,0:T(8,128)(2,1)}, bf16[128,2048]{1,0:T(8,128)(2,1)}, bf16[16,128]{1,0:T(8,128)(2,1)}) custom-call(bf16[392,128]{1,0:T(8,128)(2,1)S(1)} %gain.1.refs_0_, bf16[392,128]{1,0:T(8,128)(2,1)S(1)} %collective-permute-done.3.refs_1_.refs_0_, ...), custom_call_target="tpu_custom_call" | custom-call | tf_op jit(solution)/shard_map/place/pallas_call | solution.py:159
  (22 shorter events, 0.2 us)
Async XLA Ops:
  1.5 6.1 %collective-permute-start.2 = (bf16[8,128]{1,0:T(8,128)(2,1)S(1)}, bf16[8,128]{1,0:T(8,128)(2,1)S(1)}, u32[]{:S(2)}, u32[]{:S(2)}) collective-permute-start(bf16[8,128]{1,0:T(8,128)(2,1)S(1)} %fusion.2.own), channel_id=1, source_target_pairs={{0,6},{2,0},{4,2},{6,4},{1,7},{3,1},{5,3},{7,5},{8,14},{10,8},{12,... | collective-permute-start | bytes 6152 | tf_op jit(solution)/shard_map/ppermute | solution.py:131
  3.7 5.1 %collective-permute-start.1 = (bf16[8,128]{1,0:T(8,128)(2,1)S(1)}, bf16[8,128]{1,0:T(8,128)(2,1)S(1)}, u32[]{:S(2)}, u32[]{:S(2)}) collective-permute-start(bf16[8,128]{1,0:T(8,128)(2,1)S(1)} %fusion.2.own), channel_id=1, source_target_pairs={{0,4},{2,6},{4,0},{6,2},{1,5},{3,7},{5,1},{7,3},{8,12},{10,14},{12... | collective-permute-start | bytes 6152 | tf_op jit(solution)/shard_map/ppermute | solution.py:131
  4.6 4.2 %collective-permute-start = (bf16[8,128]{1,0:T(8,128)(2,1)S(1)}, bf16[8,128]{1,0:T(8,128)(2,1)S(1)}, u32[]{:S(2)}, u32[]{:S(2)}) collective-permute-start(bf16[8,128]{1,0:T(8,128)(2,1)S(1)} %fusion.2.own), channel_id=1, source_target_pairs={{0,2},{2,4},{4,6},{6,0},{1,3},{3,5},{5,7},{7,1},{8,10},{10,12},{12... | collective-permute-start | bytes 6152 | tf_op jit(solution)/shard_map/ppermute | solution.py:131
  8.8 9.4 %collective-permute-start.3 = (bf16[392,128]{1,0:T(8,128)(2,1)S(1)}, bf16[392,128]{1,0:T(8,128)(2,1)S(1)}, u32[]{:S(2)}, u32[]{:S(2)}) collective-permute-start(bf16[392,128]{1,0:T(8,128)(2,1)S(1)} %gain.1.refs_0_), channel_id=1, source_target_pairs={{128,0},{136,8},{144,16},{152,24},{160,32},{168,40},{176,48},{184,... | collective-permute-start | bytes 301064 | tf_op jit(solution)/shard_map/ppermute | solution.py:45
  15.4 12.3 %collective-permute-start.5 = (bf16[392,128]{1,0:T(8,128)(2,1)S(1)}, bf16[392,128]{1,0:T(8,128)(2,1)S(1)}, u32[]{:S(2)}, u32[]{:S(2)}) collective-permute-start(bf16[392,128]{1,0:T(8,128)(2,1)S(1)} %gain.1.refs_0_), channel_id=1, source_target_pairs={{80,0},{88,8},{64,16},{72,24},{112,32},{120,40},{96,48},{104,56},{... | collective-permute-start | bytes 301064 | tf_op jit(solution)/shard_map/ppermute | solution.py:45
  18.2 18.8 %collective-permute-start.8 = (bf16[784,128]{1,0:T(8,128)(2,1)S(1)}, bf16[784,128]{1,0:T(8,128)(2,1)S(1)}, u32[]{:S(2)}, u32[]{:S(2)}) collective-permute-start(bf16[784,128]{1,0:T(8,128)(2,1)S(1)} %pack.7), channel_id=1, source_target_pairs={{8,0},{16,8},{24,16},{0,24},{40,32},{48,40},{56,48},{32,56},{72,64... | collective-permute-start | bytes 602120 | tf_op jit(solution)/shard_map/ppermute | solution.py:45
  21.0 16.7 %collective-permute-start.7 = (bf16[784,128]{1,0:T(8,128)(2,1)S(1)}, bf16[784,128]{1,0:T(8,128)(2,1)S(1)}, u32[]{:S(2)}, u32[]{:S(2)}) collective-permute-start(bf16[784,128]{1,0:T(8,128)(2,1)S(1)} %pack.7), channel_id=1, source_target_pairs={{32,0},{40,8},{48,16},{56,24},{64,32},{72,40},{80,48},{88,56},{96,... | collective-permute-start | bytes 602120 | tf_op jit(solution)/shard_map/ppermute | solution.py:45
  27.6 9.3 %collective-permute-start.6 = (bf16[392,128]{1,0:T(8,128)(2,1)S(1)}, bf16[392,128]{1,0:T(8,128)(2,1)S(1)}, u32[]{:S(2)}, u32[]{:S(2)}) collective-permute-start(bf16[392,128]{1,0:T(8,128)(2,1)S(1)} %gain.1.refs_0_), channel_id=1, source_target_pairs={{208,0},{216,8},{192,16},{200,24},{240,32},{248,40},{224,48},{232,... | collective-permute-start | bytes 301064 | tf_op jit(solution)/shard_map/ppermute | solution.py:45
  27.6 9.3 %collective-permute-start.4 = (bf16[392,128]{1,0:T(8,128)(2,1)S(1)}, bf16[392,128]{1,0:T(8,128)(2,1)S(1)}, u32[]{:S(2)}, u32[]{:S(2)}) collective-permute-start(bf16[392,128]{1,0:T(8,128)(2,1)S(1)} %gain.1.refs_0_), channel_id=1, source_target_pairs={{224,0},{232,8},{240,16},{248,24},{0,32},{8,40},{16,48},{24,56},{3... | collective-permute-start | bytes 301064 | tf_op jit(solution)/shard_map/ppermute | solution.py:45
  27.7 11.6 %collective-permute-start.9 = (bf16[784,128]{1,0:T(8,128)(2,1)S(1)}, bf16[784,128]{1,0:T(8,128)(2,1)S(1)}, u32[]{:S(2)}, u32[]{:S(2)}) collective-permute-start(bf16[784,128]{1,0:T(8,128)(2,1)S(1)} %pack.8), channel_id=1, source_target_pairs={{24,0},{0,8},{8,16},{16,24},{56,32},{32,40},{40,48},{48,56},{88,64... | collective-permute-start | bytes 602120 | tf_op jit(solution)/shard_map/ppermute | solution.py:45
  37.0 16.0 %collective-permute-start.12 = (bf16[1960,128]{1,0:T(8,128)(2,1)S(1)}, bf16[1960,128]{1,0:T(8,128)(2,1)S(1)}, u32[]{:S(2)}, u32[]{:S(2)}) collective-permute-start(bf16[1960,128]{1,0:T(8,128)(2,1)S(1)} %pack.11), channel_id=1, source_target_pairs={{8,0},{16,8},{24,16},{0,24},{40,32},{48,40},{56,48},{32,56},{72,64... | collective-permute-start | bytes 1505288 | tf_op jit(solution)/shard_map/ppermute | solution.py:45
  37.8 15.3 %collective-permute-start.11 = (bf16[1960,128]{1,0:T(8,128)(2,1)S(1)}, bf16[1960,128]{1,0:T(8,128)(2,1)S(1)}, u32[]{:S(2)}, u32[]{:S(2)}) collective-permute-start(bf16[1960,128]{1,0:T(8,128)(2,1)S(1)} %pack.10), channel_id=1, source_target_pairs={{24,0},{0,8},{8,16},{16,24},{56,32},{32,40},{40,48},{48,56},{88,64... | collective-permute-start | bytes 1505288 | tf_op jit(solution)/shard_map/ppermute | solution.py:45
  39.3 13.7 %collective-permute-start.14 = (bf16[1568,128]{1,0:T(8,128)(2,1)S(1)}, bf16[1568,128]{1,0:T(8,128)(2,1)S(1)}, u32[]{:S(2)}, u32[]{:S(2)}) collective-permute-start(bf16[1568,128]{1,0:T(8,128)(2,1)S(1)} %pack.13), channel_id=1, source_target_pairs={{224,0},{232,8},{240,16},{248,24},{0,32},{8,40},{16,48},{24,56},{3... | collective-permute-start | bytes 1204232 | tf_op jit(solution)/shard_map/ppermute | solution.py:45
  39.4 13.6 %collective-permute-start.13 = (bf16[1568,128]{1,0:T(8,128)(2,1)S(1)}, bf16[1568,128]{1,0:T(8,128)(2,1)S(1)}, u32[]{:S(2)}, u32[]{:S(2)}) collective-permute-start(bf16[1568,128]{1,0:T(8,128)(2,1)S(1)} %pack.12), channel_id=1, source_target_pairs={{32,0},{40,8},{48,16},{56,24},{64,32},{72,40},{80,48},{88,56},{96,... | collective-permute-start | bytes 1204232 | tf_op jit(solution)/shard_map/ppermute | solution.py:45
  42.7 10.3 %collective-permute-start.10 = (bf16[1176,128]{1,0:T(8,128)(2,1)S(1)}, bf16[1176,128]{1,0:T(8,128)(2,1)S(1)}, u32[]{:S(2)}, u32[]{:S(2)}) collective-permute-start(bf16[1176,128]{1,0:T(8,128)(2,1)S(1)} %pack.9), channel_id=1, source_target_pairs={{224,0},{232,8},{240,16},{248,24},{0,32},{8,40},{16,48},{24,56},{3... | collective-permute-start | bytes 903176 | tf_op jit(solution)/shard_map/ppermute | solution.py:45

commit v2 on v1

--- a/solution.py
+++ b/solution.py
@@ -20,19 +20,22 @@
 WEIGHT_ROWS = CHUNKS * BLOCK
 SENT_ROWS = WEIGHT_ROWS + 8
 
+FIRST, LAST = (0, CHUNKS // 2), (CHUNKS // 2, CHUNKS)
+WHOLE = (FIRST, LAST)
 STEPS = (
-    ((4, 0), ((0, 0),)),
-    ((7, 0), ((0, 0),)),
-    ((2, 2), ((0, 0),)),
-    ((6, 2), ((0, 0),)),
-    ((1, 0), ((0, 0), (4, 0))),
-    ((0, 1), ((0, 0), (4, 0))),
-    ((0, -1), ((2, 2), (4, 0))),
-    ((-1, 0), ((2, 2), (4, 0), (7, 0))),
-    ((0, -1), ((0, 0), (1, 0), (5, 0), (6, 2), (7, 0))),
-    ((0, 1), ((0, 1), (2, 2), (4, 1), (6, 2), (7, 0))),
-    ((1, 0), ((1, 0), (2, 2), (4, 1), (6, 2))),
-    ((-1, 0), ((2, 1), (4, 1), (4, 3), (6, 2))),
+    ((4, 0), ((0, 0, WHOLE),)),
+    ((2, 2), ((0, 0, WHOLE),)),
+    ((7, 0), ((0, 0, WHOLE),)),
+    ((6, 2), ((0, 0, WHOLE),)),
+    ((1, 0), ((0, 0, WHOLE),)),
+    ((0, -1), ((4, 0, WHOLE), (7, 0, WHOLE),)),
+    ((0, 1), ((0, 0, WHOLE), (4, 0, WHOLE),)),
+    ((1, 0), ((1, 0, WHOLE), (2, 2, WHOLE), (4, 0, WHOLE),)),
+    ((-1, 0), ((2, 2, WHOLE), (4, 0, WHOLE), (7, 0, WHOLE),)),
+    ((0, -1), ((0, 0, WHOLE), (1, 0, WHOLE), (2, 2, WHOLE), (4, 3, (LAST,)), (6, 2, WHOLE), (7, 3, (FIRST,)),)),
+    ((0, 1), ((0, 1, WHOLE), (2, 2, WHOLE), (4, 1, (FIRST,)), (6, 2, WHOLE), (7, 0, WHOLE),)),
+    ((1, 0), ((0, 1, WHOLE), (4, 1, WHOLE), (4, 3, WHOLE), (6, 2, (LAST,)),)),
+    ((-1, 0), ((4, 1, WHOLE), (4, 3, WHOLE), (6, 2, WHOLE),)),
 )
 
 
@@ -62,20 +65,27 @@
     out[WEIGHT_ROWS:, :] = own[...] + first[...] + second[...] + third[...]
 
 
+def size_of(half):
+    first, last = half
+    return (last - first) * BLOCK + (SENT_ROWS - WEIGHT_ROWS if last == CHUNKS else 0)
+
+
 def pack(sent, parts):
-    if len(parts) == 1 and sent[parts[0][0]].shape[0] == SENT_ROWS:
+    total = sum(size for _, _, size in parts)
+    if len({at for at, _, _ in parts}) == 1 and sent[parts[0][0]].shape[0] == total:
         return sent[parts[0][0]]
-    used = sorted({at for at, _ in parts})
+    used = sorted({at for at, _, _ in parts})
 
     def kernel(*refs):
-        for number, (at, row) in enumerate(parts):
-            to = number * SENT_ROWS
-            refs[-1][to : to + SENT_ROWS, :] = refs[used.index(at)][row : row + SENT_ROWS, :]
+        to = 0
+        for at, row, size in parts:
+            refs[-1][to : to + size, :] = refs[used.index(at)][row : row + size, :]
+            to += size
 
     vmem = pl.BlockSpec(memory_space=pltpu.VMEM)
     return pl.pallas_call(
         kernel,
-        out_shape=pltpu.VMEM((len(parts) * SENT_ROWS, LANES), jnp.bfloat16),
+        out_shape=pltpu.VMEM((total, LANES), jnp.bfloat16),
         in_specs=[vmem] * len(used),
         out_specs=vmem,
         compiler_params=pltpu.CompilerParams(vmem_limit_bytes=2**20),
@@ -87,18 +97,16 @@
     n = 1 + max(p[0] for p in pieces)
     sent, (query, key, value, norm), (rows, tiles, turned, sems) = refs[:n], refs[n : n + 4], refs[n + 4 :]
     z, x = lax.axis_index("rows_0"), lax.axis_index("rows_1")
-    for at, row, (dz, dx) in pieces:
-        rank = lax.rem(z + dz % RING_0, RING_0) * RING_1 + lax.rem(x + dx % RING_1, RING_1)
-        start = pl.multiple_of(rank * BLOCK, BLOCK)
-        for chunk in range(CHUNKS):
-            rows[chunk, pl.ds(start, BLOCK), :] = sent[at][row + chunk * BLOCK : row + (chunk + 1) * BLOCK, :]
-        tiles[rank] = sent[at][row + WEIGHT_ROWS : row + SENT_ROWS, :].astype(jnp.float32)
-    lane = lax.broadcasted_iota(jnp.int32, (1, LANES), 1)
-    for pair in range(RANKS // 2):
-        both = jnp.where(lane < BLOCK, tiles[2 * pair, 0:1, :], tiles[2 * pair + 1, 0:1, :])
-        norm[pair : pair + 1, :] = both.astype(jnp.bfloat16)
+    placed = []
+    for at, row, (first, last), (dz, dx) in pieces:
+        rank = lax.rem(z + dz, RING_0) * RING_1 + lax.rem(x + dx, RING_1)
+        placed.append((sent[at], row, first, last, rank))
     copies = []
     for chunk in range(CHUNKS):
+        for block, row, first, last, rank in placed:
+            if first <= chunk < last:
+                at = row + (chunk - first) * BLOCK
+                rows[chunk, pl.ds(pl.multiple_of(rank * BLOCK, BLOCK), BLOCK), :] = block[at : at + BLOCK, :]
         for tile in range(RANKS * BLOCK // LANES):
             lanes = slice(tile * LANES, (tile + 1) * LANES)
             turned[chunk, :, lanes] = rows[chunk, lanes, :].T
@@ -107,6 +115,14 @@
             pltpu.make_async_copy(turned.at[chunk], out.at[row * LANES : (row + 1) * LANES, :], sems.at[chunk])
         )
         copies[-1].start()
+    for block, row, first, last, rank in placed:
+        if last == CHUNKS:
+            at = row + (last - first) * BLOCK
+            tiles[rank] = block[at : at + 8, :].astype(jnp.float32)
+    lane = lax.broadcasted_iota(jnp.int32, (1, LANES), 1)
+    for pair in range(RANKS // 2):
+        both = jnp.where(lane < BLOCK, tiles[2 * pair, 0:1, :], tiles[2 * pair + 1, 0:1, :])
+        norm[pair : pair + 1, :] = both.astype(jnp.bfloat16)
     for copy in copies:
         copy.wait()
 
@@ -145,14 +161,19 @@
         name="gain",
     )(*(pltpu.with_memory_space_constraint(a, pltpu.VMEM) for a in (block, gain, *others)))
 
-    sent, held = [block], {(0, 0): (0, 0)}
+    sent = [block]
+    held = {(0, 0, FIRST): (0, 0), (0, 0, LAST): (0, size_of(FIRST))}
     for offset, passed in STEPS:
-        arrived = from_offset(pack(sent, [held[p] for p in passed]), *offset)
-        for place, (dz, dx) in enumerate(passed):
-            held[(offset[0] + dz) % RING_0, (offset[1] + dx) % RING_1] = (len(sent), place * SENT_ROWS)
-        sent.append(arrived)
-    pieces = [(at, row, offset) for offset, (at, row) in held.items()]
-    assert len(pieces) == RANKS == 1 + sum(len(passed) for _, passed in STEPS)
+        parts, row = [], 0
+        for dz, dx, halves in passed:
+            for half in halves:
+                at, start = held[dz, dx, half]
+                parts.append((at, start, size_of(half)))
+                held[(offset[0] + dz) % RING_0, (offset[1] + dx) % RING_1, half] = (len(sent), row)
+                row += size_of(half)
+        sent.append(from_offset(pack(sent, parts), *offset))
+    pieces = [(at, row, half, (dz, dx)) for (dz, dx, half), (at, row) in held.items()]
+    assert len(pieces) == 2 * RANKS == 2 + sum(len(halves) for _, passed in STEPS for _, _, halves in passed)
 
     hbm = pl.BlockSpec(memory_space=pl.ANY)
     width = RANKS * BLOCK

time: 55.9 us -> 62.8 us (1.12)
  waiting for transfers between devices: 21.2 us -> 29.3 us
  starting transfers between devices: 29 us -> 27.7 us
    ppermute x12 -> x13, waiting for transfers between devices: 20 us -> 28.1 us  [from_offset(): return lax.ppermute(array, ROWS, pairs)]
    ppermute x12 -> x13, starting transfers between devices: 24 us -> 22.7 us  [from_offset(): return lax.ppermute(array, ROWS, pairs)]
  transfers between devices with their start and end apart: 15 -> 16, of which waited for: 4 -> 6; matrix products, arithmetic and copies ran while one was open for 0% -> 0% of each run, Pallas kernels for 2% -> 2%
where the time goes in v2:
time: 62.8 us; the launch traced here: 62.5 us
  waiting for transfers between devices  29.3 us (47%)
  starting transfers between devices  27.7 us (44%)
  Pallas kernels  3.93 us (6%)
  between operations  0.73 us (1%)
  other arithmetic  0.71 us (1%)
    ppermute x13, waiting for transfers between devices, from_offset(): return lax.ppermute(array, ROWS, pairs)  28.1 us
    ppermute x13, starting transfers between devices, from_offset(): return lax.ppermute(array, ROWS, pairs)  22.7 us
    ppermute x3, starting transfers between devices, shards(): lax.ppermute(gain, 'tp', [(i, (i + s) % TP) for i in range(TP)])  5 us
    pallas_call x1, Pallas kernels, shards(): pl.pallas_call(lambda *refs: place_kernel(pieces, *refs), out_shape=(jax....  2.64 us
  transfers between devices with their start and end apart: 16, of which 6 were waited for; matrix products, arithmetic and copies ran while one was open for 0% of the time, Pallas kernels for 2%

profile of v2, /device:TPU:8, one launch (start us, length us, event | category | flops | bytes accessed | tf_op | source)
XLA Modules:
  0.0 62.5 jit_solution(1561815051673948722)
XLA Ops:
  0.7 0.7 %add_convert_fusion = bf16[16]{0:T(256)(128)(2,1)S(1)} fusion(f32[16]{0:T(128)} %param.20, f32[16]{0:T(128)} %param.21), kind=kLoop, calls=%fused_computation.12 | loop fusion | flops 32 | bytes 160 | tf_op jit(solution)/shard_map/convert_element_type | solution.py:144
  1.5 2.2 %collective-permute-start.2 = (bf16[8,128]{1,0:T(8,128)(2,1)S(1)}, bf16[8,128]{1,0:T(8,128)(2,1)S(1)}, u32[]{:S(2)}, u32[]{:S(2)}) collective-permute-start(bf16[8,128]{1,0:T(8,128)(2,1)S(1)} %fusion.2.own), channel_id=1, source_target_pairs={{0,6},{2,0},{4,2},{6,4},{1,7},{3,1},{5,3},{7,5},{8,14},{10,8},{12,... | collective-permute-start | bytes 6152 | tf_op jit(solution)/shard_map/ppermute | solution.py:147
  3.7 0.9 %collective-permute-start.1 = (bf16[8,128]{1,0:T(8,128)(2,1)S(1)}, bf16[8,128]{1,0:T(8,128)(2,1)S(1)}, u32[]{:S(2)}, u32[]{:S(2)}) collective-permute-start(bf16[8,128]{1,0:T(8,128)(2,1)S(1)} %fusion.2.own), channel_id=1, source_target_pairs={{0,4},{2,6},{4,0},{6,2},{1,5},{3,7},{5,1},{7,3},{8,12},{10,14},{12... | collective-permute-start | bytes 6152 | tf_op jit(solution)/shard_map/ppermute | solution.py:147
  4.6 1.9 %collective-permute-start = (bf16[8,128]{1,0:T(8,128)(2,1)S(1)}, bf16[8,128]{1,0:T(8,128)(2,1)S(1)}, u32[]{:S(2)}, u32[]{:S(2)}) collective-permute-start(bf16[8,128]{1,0:T(8,128)(2,1)S(1)} %fusion.2.own), channel_id=1, source_target_pairs={{0,2},{2,4},{4,6},{6,0},{1,3},{3,5},{5,7},{7,1},{8,10},{10,12},{12... | collective-permute-start | bytes 6152 | tf_op jit(solution)/shard_map/ppermute | solution.py:147
  6.5 1.1 %merge.1._ = bf16[392,128]{1,0:T(8,128)(2,1)S(1)} custom-call(bf16[64,512]{1,0:T(8,128)(2,1)} %tq.1, bf16[64,64]{1,0:T(8,128)(2,1)} %lq.1, bf16[64,512]{1,0:T(8,128)(2,1)} %hq.1, bf16[64,128]{1,0:T(8,128)(2,1)} %tk.1, bf16[64,64]{1,0:T(8,128)(2,1)} %lk.1, bf16[64,128]{1,0:T(8,128)(2,1)} %hk.1, bf16[64,128]{1,0:T(8,128)(2,1)} %tv.1, bf16[64,64]{1,0:T(8,128)(2,1)} %lv.1, ...), custom_call_target="tpu_custom_call" | custom-call | tf_op jit(solution)/shard_map/merge/pallas_call | solution.py:148
  7.6 1.2 %collective-permute-done.1.second = bf16[8,128]{1,0:T(8,128)(2,1)S(1)} collective-permute-done((bf16[8,128]{1,0:T(8,128)(2,1)S(1)}, bf16[8,128]{1,0:T(8,128)(2,1)S(1)}, u32[]{:S(2)}, u32[]{:S(2)}) %collective-permute-start.1) | collective-permute-done | bytes 2080 | tf_op jit(solution)/shard_map/ppermute | solution.py:147
  8.8 1.3 %collective-permute-start.5 = (bf16[392,128]{1,0:T(8,128)(2,1)S(1)}, bf16[392,128]{1,0:T(8,128)(2,1)S(1)}, u32[]{:S(2)}, u32[]{:S(2)}) collective-permute-start(bf16[392,128]{1,0:T(8,128)(2,1)S(1)} %gain.1.refs_0_), channel_id=1, source_target_pairs={{224,0},{232,8},{240,16},{248,24},{0,32},{8,40},{16,48},{24,56},{3... | collective-permute-start | bytes 301064 | tf_op jit(solution)/shard_map/ppermute | solution.py:48
  10.1 6.3 %collective-permute-start.3 = (bf16[392,128]{1,0:T(8,128)(2,1)S(1)}, bf16[392,128]{1,0:T(8,128)(2,1)S(1)}, u32[]{:S(2)}, u32[]{:S(2)}) collective-permute-start(bf16[392,128]{1,0:T(8,128)(2,1)S(1)} %gain.1.refs_0_), channel_id=1, source_target_pairs={{128,0},{136,8},{144,16},{152,24},{160,32},{168,40},{176,48},{184,... | collective-permute-start | bytes 301064 | tf_op jit(solution)/shard_map/ppermute | solution.py:48
  16.4 2.2 %collective-permute-start.7 = (bf16[392,128]{1,0:T(8,128)(2,1)S(1)}, bf16[392,128]{1,0:T(8,128)(2,1)S(1)}, u32[]{:S(2)}, u32[]{:S(2)}) collective-permute-start(bf16[392,128]{1,0:T(8,128)(2,1)S(1)} %gain.1.refs_0_), channel_id=1, source_target_pairs={{32,0},{40,8},{48,16},{56,24},{64,32},{72,40},{80,48},{88,56},{96,... | collective-permute-start | bytes 301064 | tf_op jit(solution)/shard_map/ppermute | solution.py:48
  18.6 0.9 %collective-permute-start.4 = (bf16[392,128]{1,0:T(8,128)(2,1)S(1)}, bf16[392,128]{1,0:T(8,128)(2,1)S(1)}, u32[]{:S(2)}, u32[]{:S(2)}) collective-permute-start(bf16[392,128]{1,0:T(8,128)(2,1)S(1)} %gain.1.refs_0_), channel_id=1, source_target_pairs={{80,0},{88,8},{64,16},{72,24},{112,32},{120,40},{96,48},{104,56},{... | collective-permute-start | bytes 301064 | tf_op jit(solution)/shard_map/ppermute | solution.py:48
  19.5 1.6 %collective-permute-done.3.refs_0_.refs_1_ = bf16[392,128]{1,0:T(8,128)(2,1)S(1)} collective-permute-done((bf16[392,128]{1,0:T(8,128)(2,1)S(1)}, bf16[392,128]{1,0:T(8,128)(2,1)S(1)}, u32[]{:S(2)}, u32[]{:S(2)}) %collective-permute-start.3) | collective-permute-done | bytes 100384 | tf_op jit(solution)/shard_map/ppermute | solution.py:48
  21.2 1.6 %collective-permute-start.8 = (bf16[784,128]{1,0:T(8,128)(2,1)S(1)}, bf16[784,128]{1,0:T(8,128)(2,1)S(1)}, u32[]{:S(2)}, u32[]{:S(2)}) collective-permute-start(bf16[784,128]{1,0:T(8,128)(2,1)S(1)} %pack.8), channel_id=1, source_target_pairs={{24,0},{0,8},{8,16},{16,24},{56,32},{32,40},{40,48},{48,56},{88,64... | collective-permute-start | bytes 602120 | tf_op jit(solution)/shard_map/ppermute | solution.py:48
  22.7 1.8 %collective-permute-start.9 = (bf16[784,128]{1,0:T(8,128)(2,1)S(1)}, bf16[784,128]{1,0:T(8,128)(2,1)S(1)}, u32[]{:S(2)}, u32[]{:S(2)}) collective-permute-start(bf16[784,128]{1,0:T(8,128)(2,1)S(1)} %pack.9), channel_id=1, source_target_pairs={{8,0},{16,8},{24,16},{0,24},{40,32},{48,40},{56,48},{32,56},{72,64... | collective-permute-start | bytes 602120 | tf_op jit(solution)/shard_map/ppermute | solution.py:48
  24.6 4.9 %collective-permute-done.4.refs_1_.refs_0_.refs_2_ = bf16[392,128]{1,0:T(8,128)(2,1)S(1)} collective-permute-done((bf16[392,128]{1,0:T(8,128)(2,1)S(1)}, bf16[392,128]{1,0:T(8,128)(2,1)S(1)}, u32[]{:S(2)}, u32[]{:S(2)}) %collective-permute-start.4) | collective-permute-done | bytes 100384 | tf_op jit(solution)/shard_map/ppermute | solution.py:48
  29.5 1.4 %collective-permute-start.10 = (bf16[1176,128]{1,0:T(8,128)(2,1)S(1)}, bf16[1176,128]{1,0:T(8,128)(2,1)S(1)}, u32[]{:S(2)}, u32[]{:S(2)}) collective-permute-start(bf16[1176,128]{1,0:T(8,128)(2,1)S(1)} %pack.10), channel_id=1, source_target_pairs={{32,0},{40,8},{48,16},{56,24},{64,32},{72,40},{80,48},{88,56},{96,... | collective-permute-start | bytes 903176 | tf_op jit(solution)/shard_map/ppermute | solution.py:48
  30.9 1.5 %collective-permute-start.6 = (bf16[392,128]{1,0:T(8,128)(2,1)S(1)}, bf16[392,128]{1,0:T(8,128)(2,1)S(1)}, u32[]{:S(2)}, u32[]{:S(2)}) collective-permute-start(bf16[392,128]{1,0:T(8,128)(2,1)S(1)} %gain.1.refs_0_), channel_id=1, source_target_pairs={{208,0},{216,8},{192,16},{200,24},{240,32},{248,40},{224,48},{232,... | collective-permute-start | bytes 301064 | tf_op jit(solution)/shard_map/ppermute | solution.py:48
  32.5 8.5 %collective-permute-done.6.refs_2_.refs_0_.refs_4_ = bf16[392,128]{1,0:T(8,128)(2,1)S(1)} collective-permute-done((bf16[392,128]{1,0:T(8,128)(2,1)S(1)}, bf16[392,128]{1,0:T(8,128)(2,1)S(1)}, u32[]{:S(2)}, u32[]{:S(2)}) %collective-permute-start.6) | collective-permute-done | bytes 100384 | tf_op jit(solution)/shard_map/ppermute | solution.py:48
  41.0 0.7 %collective-permute-start.12 = (bf16[1960,128]{1,0:T(8,128)(2,1)S(1)}, bf16[1960,128]{1,0:T(8,128)(2,1)S(1)}, u32[]{:S(2)}, u32[]{:S(2)}) collective-permute-start(bf16[1960,128]{1,0:T(8,128)(2,1)S(1)} %pack.12), channel_id=1, source_target_pairs={{24,0},{0,8},{8,16},{16,24},{56,32},{32,40},{40,48},{48,56},{88,64... | collective-permute-start | bytes 1505288 | tf_op jit(solution)/shard_map/ppermute | solution.py:48
  41.8 2.7 %collective-permute-start.13 = (bf16[1760,128]{1,0:T(8,128)(2,1)S(1)}, bf16[1760,128]{1,0:T(8,128)(2,1)S(1)}, u32[]{:S(2)}, u32[]{:S(2)}) collective-permute-start(bf16[1760,128]{1,0:T(8,128)(2,1)S(1)} %pack.13), channel_id=1, source_target_pairs={{8,0},{16,8},{24,16},{0,24},{40,32},{48,40},{56,48},{32,56},{72,64... | collective-permute-start | bytes 1351688 | tf_op jit(solution)/shard_map/ppermute | solution.py:48
  44.5 1.7 %collective-permute-start.14 = (bf16[1376,128]{1,0:T(8,128)(2,1)S(1)}, bf16[1376,128]{1,0:T(8,128)(2,1)S(1)}, u32[]{:S(2)}, u32[]{:S(2)}) collective-permute-start(bf16[1376,128]{1,0:T(8,128)(2,1)S(1)} %pack.14), channel_id=1, source_target_pairs={{32,0},{40,8},{48,16},{56,24},{64,32},{72,40},{80,48},{88,56},{96,... | collective-permute-start | bytes 1056776 | tf_op jit(solution)/shard_map/ppermute | solution.py:48
  46.2 0.5 collective-permute-start.11
  46.8 9.8 %collective-permute-done.11.refs_9_ = bf16[1176,128]{1,0:T(8,128)(2,1)S(1)} collective-permute-done((bf16[1176,128]{1,0:T(8,128)(2,1)S(1)}, bf16[1176,128]{1,0:T(8,128)(2,1)S(1)}, u32[]{:S(2)}, u32[]{:S(2)}) %collective-permute-start.11) | collective-permute-done | bytes 301088 | tf_op jit(solution)/shard_map/ppermute | solution.py:48
  56.6 3.2 %collective-permute-done.15.refs_13_ = bf16[1176,128]{1,0:T(8,128)(2,1)S(1)} collective-permute-done((bf16[1176,128]{1,0:T(8,128)(2,1)S(1)}, bf16[1176,128]{1,0:T(8,128)(2,1)S(1)}, u32[]{:S(2)}, u32[]{:S(2)}) %collective-permute-start.15) | collective-permute-done | bytes 301088 | tf_op jit(solution)/shard_map/ppermute | solution.py:48
  59.8 2.6 %place.1 = (bf16[512,2048]{1,0:T(8,128)(2,1)}, bf16[128,2048]{1,0:T(8,128)(2,1)}, bf16[128,2048]{1,0:T(8,128)(2,1)}, bf16[16,128]{1,0:T(8,128)(2,1)}) custom-call(bf16[392,128]{1,0:T(8,128)(2,1)S(1)} %gain.1.refs_0_, bf16[392,128]{1,0:T(8,128)(2,1)S(1)} %collective-permute-done.3.refs_0_.refs_1_, ...), custom_call_target="tpu_custom_call" | custom-call | tf_op jit(solution)/shard_map/place/pallas_call | solution.py:180
  (25 shorter events, 0.4 us)
Async XLA Ops:
  1.5 6.1 %collective-permute-start.2 = (bf16[8,128]{1,0:T(8,128)(2,1)S(1)}, bf16[8,128]{1,0:T(8,128)(2,1)S(1)}, u32[]{:S(2)}, u32[]{:S(2)}) collective-permute-start(bf16[8,128]{1,0:T(8,128)(2,1)S(1)} %fusion.2.own), channel_id=1, source_target_pairs={{0,6},{2,0},{4,2},{6,4},{1,7},{3,1},{5,3},{7,5},{8,14},{10,8},{12,... | collective-permute-start | bytes 6152 | tf_op jit(solution)/shard_map/ppermute | solution.py:147
  3.7 5.1 %collective-permute-start.1 = (bf16[8,128]{1,0:T(8,128)(2,1)S(1)}, bf16[8,128]{1,0:T(8,128)(2,1)S(1)}, u32[]{:S(2)}, u32[]{:S(2)}) collective-permute-start(bf16[8,128]{1,0:T(8,128)(2,1)S(1)} %fusion.2.own), channel_id=1, source_target_pairs={{0,4},{2,6},{4,0},{6,2},{1,5},{3,7},{5,1},{7,3},{8,12},{10,14},{12... | collective-permute-start | bytes 6152 | tf_op jit(solution)/shard_map/ppermute | solution.py:147
  4.6 4.2 %collective-permute-start = (bf16[8,128]{1,0:T(8,128)(2,1)S(1)}, bf16[8,128]{1,0:T(8,128)(2,1)S(1)}, u32[]{:S(2)}, u32[]{:S(2)}) collective-permute-start(bf16[8,128]{1,0:T(8,128)(2,1)S(1)} %fusion.2.own), channel_id=1, source_target_pairs={{0,2},{2,4},{4,6},{6,0},{1,3},{3,5},{5,7},{7,1},{8,10},{10,12},{12... | collective-permute-start | bytes 6152 | tf_op jit(solution)/shard_map/ppermute | solution.py:147
  8.8 10.7 %collective-permute-start.5 = (bf16[392,128]{1,0:T(8,128)(2,1)S(1)}, bf16[392,128]{1,0:T(8,128)(2,1)S(1)}, u32[]{:S(2)}, u32[]{:S(2)}) collective-permute-start(bf16[392,128]{1,0:T(8,128)(2,1)S(1)} %gain.1.refs_0_), channel_id=1, source_target_pairs={{224,0},{232,8},{240,16},{248,24},{0,32},{8,40},{16,48},{24,56},{3... | collective-permute-start | bytes 301064 | tf_op jit(solution)/shard_map/ppermute | solution.py:48
  10.1 11.1 %collective-permute-start.3 = (bf16[392,128]{1,0:T(8,128)(2,1)S(1)}, bf16[392,128]{1,0:T(8,128)(2,1)S(1)}, u32[]{:S(2)}, u32[]{:S(2)}) collective-permute-start(bf16[392,128]{1,0:T(8,128)(2,1)S(1)} %gain.1.refs_0_), channel_id=1, source_target_pairs={{128,0},{136,8},{144,16},{152,24},{160,32},{168,40},{176,48},{184,... | collective-permute-start | bytes 301064 | tf_op jit(solution)/shard_map/ppermute | solution.py:48
  16.4 8.2 %collective-permute-start.7 = (bf16[392,128]{1,0:T(8,128)(2,1)S(1)}, bf16[392,128]{1,0:T(8,128)(2,1)S(1)}, u32[]{:S(2)}, u32[]{:S(2)}) collective-permute-start(bf16[392,128]{1,0:T(8,128)(2,1)S(1)} %gain.1.refs_0_), channel_id=1, source_target_pairs={{32,0},{40,8},{48,16},{56,24},{64,32},{72,40},{80,48},{88,56},{96,... | collective-permute-start | bytes 301064 | tf_op jit(solution)/shard_map/ppermute | solution.py:48
  18.6 10.9 %collective-permute-start.4 = (bf16[392,128]{1,0:T(8,128)(2,1)S(1)}, bf16[392,128]{1,0:T(8,128)(2,1)S(1)}, u32[]{:S(2)}, u32[]{:S(2)}) collective-permute-start(bf16[392,128]{1,0:T(8,128)(2,1)S(1)} %gain.1.refs_0_), channel_id=1, source_target_pairs={{80,0},{88,8},{64,16},{72,24},{112,32},{120,40},{96,48},{104,56},{... | collective-permute-start | bytes 301064 | tf_op jit(solution)/shard_map/ppermute | solution.py:48
  21.2 19.8 %collective-permute-start.8 = (bf16[784,128]{1,0:T(8,128)(2,1)S(1)}, bf16[784,128]{1,0:T(8,128)(2,1)S(1)}, u32[]{:S(2)}, u32[]{:S(2)}) collective-permute-start(bf16[784,128]{1,0:T(8,128)(2,1)S(1)} %pack.8), channel_id=1, source_target_pairs={{24,0},{0,8},{8,16},{16,24},{56,32},{32,40},{40,48},{48,56},{88,64... | collective-permute-start | bytes 602120 | tf_op jit(solution)/shard_map/ppermute | solution.py:48
  22.7 19.0 %collective-permute-start.9 = (bf16[784,128]{1,0:T(8,128)(2,1)S(1)}, bf16[784,128]{1,0:T(8,128)(2,1)S(1)}, u32[]{:S(2)}, u32[]{:S(2)}) collective-permute-start(bf16[784,128]{1,0:T(8,128)(2,1)S(1)} %pack.9), channel_id=1, source_target_pairs={{8,0},{16,8},{24,16},{0,24},{40,32},{48,40},{56,48},{32,56},{72,64... | collective-permute-start | bytes 602120 | tf_op jit(solution)/shard_map/ppermute | solution.py:48
  29.5 17.2 %collective-permute-start.10 = (bf16[1176,128]{1,0:T(8,128)(2,1)S(1)}, bf16[1176,128]{1,0:T(8,128)(2,1)S(1)}, u32[]{:S(2)}, u32[]{:S(2)}) collective-permute-start(bf16[1176,128]{1,0:T(8,128)(2,1)S(1)} %pack.10), channel_id=1, source_target_pairs={{32,0},{40,8},{48,16},{56,24},{64,32},{72,40},{80,48},{88,56},{96,... | collective-permute-start | bytes 903176 | tf_op jit(solution)/shard_map/ppermute | solution.py:48
  30.9 10.0 %collective-permute-start.6 = (bf16[392,128]{1,0:T(8,128)(2,1)S(1)}, bf16[392,128]{1,0:T(8,128)(2,1)S(1)}, u32[]{:S(2)}, u32[]{:S(2)}) collective-permute-start(bf16[392,128]{1,0:T(8,128)(2,1)S(1)} %gain.1.refs_0_), channel_id=1, source_target_pairs={{208,0},{216,8},{192,16},{200,24},{240,32},{248,40},{224,48},{232,... | collective-permute-start | bytes 301064 | tf_op jit(solution)/shard_map/ppermute | solution.py:48
  41.0 18.8 %collective-permute-start.12 = (bf16[1960,128]{1,0:T(8,128)(2,1)S(1)}, bf16[1960,128]{1,0:T(8,128)(2,1)S(1)}, u32[]{:S(2)}, u32[]{:S(2)}) collective-permute-start(bf16[1960,128]{1,0:T(8,128)(2,1)S(1)} %pack.12), channel_id=1, source_target_pairs={{24,0},{0,8},{8,16},{16,24},{56,32},{32,40},{40,48},{48,56},{88,64... | collective-permute-start | bytes 1505288 | tf_op jit(solution)/shard_map/ppermute | solution.py:48
  41.8 18.0 %collective-permute-start.13 = (bf16[1760,128]{1,0:T(8,128)(2,1)S(1)}, bf16[1760,128]{1,0:T(8,128)(2,1)S(1)}, u32[]{:S(2)}, u32[]{:S(2)}) collective-permute-start(bf16[1760,128]{1,0:T(8,128)(2,1)S(1)} %pack.13), channel_id=1, source_target_pairs={{8,0},{16,8},{24,16},{0,24},{40,32},{48,40},{56,48},{32,56},{72,64... | collective-permute-start | bytes 1351688 | tf_op jit(solution)/shard_map/ppermute | solution.py:48
  44.5 15.4 %collective-permute-start.14 = (bf16[1376,128]{1,0:T(8,128)(2,1)S(1)}, bf16[1376,128]{1,0:T(8,128)(2,1)S(1)}, u32[]{:S(2)}, u32[]{:S(2)}) collective-permute-start(bf16[1376,128]{1,0:T(8,128)(2,1)S(1)} %pack.14), channel_id=1, source_target_pairs={{32,0},{40,8},{48,16},{56,24},{64,32},{72,40},{80,48},{88,56},{96,... | collective-permute-start | bytes 1056776 | tf_op jit(solution)/shard_map/ppermute | solution.py:48
  46.2 10.4 %collective-permute-start.11 = (bf16[1176,128]{1,0:T(8,128)(2,1)S(1)}, bf16[1176,128]{1,0:T(8,128)(2,1)S(1)}, u32[]{:S(2)}, u32[]{:S(2)}) collective-permute-start(bf16[1176,128]{1,0:T(8,128)(2,1)S(1)} %pack.11), channel_id=1, source_target_pairs={{224,0},{232,8},{240,16},{248,24},{0,32},{8,40},{16,48},{24,56},{3... | collective-permute-start | bytes 903176 | tf_op jit(solution)/shard_map/ppermute | solution.py:48
  46.7 13.1 %collective-permute-start.15 = (bf16[1176,128]{1,0:T(8,128)(2,1)S(1)}, bf16[1176,128]{1,0:T(8,128)(2,1)S(1)}, u32[]{:S(2)}, u32[]{:S(2)}) collective-permute-start(bf16[1176,128]{1,0:T(8,128)(2,1)S(1)} %pack.15), channel_id=1, source_target_pairs={{224,0},{232,8},{240,16},{248,24},{0,32},{8,40},{16,48},{24,56},{3... | collective-permute-start | bytes 903176 | tf_op jit(solution)/shard_map/ppermute | solution.py:48

commit v3 on v2

--- a/solution.py
+++ b/solution.py
@@ -23,19 +23,19 @@
 FIRST, LAST = (0, CHUNKS // 2), (CHUNKS // 2, CHUNKS)
 WHOLE = (FIRST, LAST)
 STEPS = (
-    ((4, 0), ((0, 0, WHOLE),)),
+    ((5, 0), ((0, 0, WHOLE),)),
     ((2, 2), ((0, 0, WHOLE),)),
-    ((7, 0), ((0, 0, WHOLE),)),
     ((6, 2), ((0, 0, WHOLE),)),
     ((1, 0), ((0, 0, WHOLE),)),
-    ((0, -1), ((4, 0, WHOLE), (7, 0, WHOLE),)),
-    ((0, 1), ((0, 0, WHOLE), (4, 0, WHOLE),)),
-    ((1, 0), ((1, 0, WHOLE), (2, 2, WHOLE), (4, 0, WHOLE),)),
-    ((-1, 0), ((2, 2, WHOLE), (4, 0, WHOLE), (7, 0, WHOLE),)),
-    ((0, -1), ((0, 0, WHOLE), (1, 0, WHOLE), (2, 2, WHOLE), (4, 3, (LAST,)), (6, 2, WHOLE), (7, 3, (FIRST,)),)),
-    ((0, 1), ((0, 1, WHOLE), (2, 2, WHOLE), (4, 1, (FIRST,)), (6, 2, WHOLE), (7, 0, WHOLE),)),
-    ((1, 0), ((0, 1, WHOLE), (4, 1, WHOLE), (4, 3, WHOLE), (6, 2, (LAST,)),)),
-    ((-1, 0), ((4, 1, WHOLE), (4, 3, WHOLE), (6, 2, WHOLE),)),
+    ((0, 1), ((0, 0, WHOLE),)),
+    ((-1, 0), ((5, 0, WHOLE), (0, 0, WHOLE),)),
+    ((0, -1), ((0, 0, WHOLE), (2, 2, WHOLE), (5, 0, WHOLE),)),
+    ((1, 0), ((1, 0, WHOLE), (2, 2, WHOLE),)),
+    ((0, 1), ((0, 1, WHOLE), (2, 2, WHOLE), (5, 0, WHOLE), (6, 2, WHOLE),)),
+    ((-1, 0), ((2, 2, WHOLE), (4, 0, WHOLE), (6, 2, WHOLE), (7, 0, WHOLE), (0, 1, WHOLE),)),
+    ((0, -1), ((1, 0, WHOLE), (4, 0, WHOLE), (6, 2, WHOLE), (7, 0, WHOLE),)),
+    ((1, 0), ((0, 1, (LAST,)), (2, 1, WHOLE), (3, 2, WHOLE), (6, 2, WHOLE),)),
+    ((0, 1), ((1, 0, (FIRST,)), (3, 2, WHOLE), (4, 0, WHOLE),)),
 )
 
 

time: 62.8 us -> 54.7 us (0.87)
  the two profiles are of different devices: /device:TPU:8 before, /device:TPU:6 now
where the time goes in v3:
time: 54.7 us; the launch traced here: 54.6 us
  starting transfers between devices  30.1 us (55%)
  waiting for transfers between devices  19 us (35%)
  Pallas kernels  3.93 us (7%)
  between operations  0.77 us (1%)
  other arithmetic  0.71 us (1%)
    ppermute x13, starting transfers between devices, from_offset(): return lax.ppermute(array, ROWS, pairs)  25.4 us
    ppermute x13, waiting for transfers between devices, from_offset(): return lax.ppermute(array, ROWS, pairs)  16.3 us
    ppermute x3, starting transfers between devices, shards(): lax.ppermute(gain, 'tp', [(i, (i + s) % TP) for i in range(TP)])  4.69 us
    ppermute x3, waiting for transfers between devices, shards(): lax.ppermute(gain, 'tp', [(i, (i + s) % TP) for i in range(TP)])  2.71 us
    pallas_call x1, Pallas kernels, shards(): pl.pallas_call(lambda *refs: place_kernel(pieces, *refs), out_shape=(jax....  2.64 us
    pallas_call x1, Pallas kernels, shards(): pl.pallas_call(merge_kernel, out_shape=pltpu.VMEM((SENT_ROWS, LANES), bf1...  1.1 us
  transfers between devices with their start and end apart: 16, of which 6 were waited for; matrix products, arithmetic and copies ran while one was open for 0% of the time, Pallas kernels for 2%

profile of v3, /device:TPU:6, one launch (start us, length us, event | category | flops | bytes accessed | tf_op | source)
XLA Modules:
  0.0 54.6 jit_solution(16841676619868624224)
XLA Ops:
  0.7 0.7 %add_convert_fusion = bf16[16]{0:T(256)(128)(2,1)S(1)} fusion(f32[16]{0:T(128)} %param.20, f32[16]{0:T(128)} %param.21), kind=kLoop, calls=%fused_computation.12 | loop fusion | flops 32 | bytes 160 | tf_op jit(solution)/shard_map/convert_element_type | solution.py:144
  1.3 0.1 broadcast_in_dim.14
  1.5 3.1 %collective-permute-start.2 = (bf16[8,128]{1,0:T(8,128)(2,1)S(1)}, bf16[8,128]{1,0:T(8,128)(2,1)S(1)}, u32[]{:S(2)}, u32[]{:S(2)}) collective-permute-start(bf16[8,128]{1,0:T(8,128)(2,1)S(1)} %fusion.2.own), channel_id=1, source_target_pairs={{0,6},{2,0},{4,2},{6,4},{1,7},{3,1},{5,3},{7,5},{8,14},{10,8},{12,... | collective-permute-start | bytes 6152 | tf_op jit(solution)/shard_map/ppermute | solution.py:147
  4.5 0.6 %collective-permute-start.1 = (bf16[8,128]{1,0:T(8,128)(2,1)S(1)}, bf16[8,128]{1,0:T(8,128)(2,1)S(1)}, u32[]{:S(2)}, u32[]{:S(2)}) collective-permute-start(bf16[8,128]{1,0:T(8,128)(2,1)S(1)} %fusion.2.own), channel_id=1, source_target_pairs={{0,4},{2,6},{4,0},{6,2},{1,5},{3,7},{5,1},{7,3},{8,12},{10,14},{12... | collective-permute-start | bytes 6152 | tf_op jit(solution)/shard_map/ppermute | solution.py:147
  5.2 1.0 %collective-permute-start = (bf16[8,128]{1,0:T(8,128)(2,1)S(1)}, bf16[8,128]{1,0:T(8,128)(2,1)S(1)}, u32[]{:S(2)}, u32[]{:S(2)}) collective-permute-start(bf16[8,128]{1,0:T(8,128)(2,1)S(1)} %fusion.2.own), channel_id=1, source_target_pairs={{0,2},{2,4},{4,6},{6,0},{1,3},{3,5},{5,7},{7,1},{8,10},{10,12},{12... | collective-permute-start | bytes 6152 | tf_op jit(solution)/shard_map/ppermute | solution.py:147
  6.1 1.1 %merge.1._ = bf16[392,128]{1,0:T(8,128)(2,1)S(1)} custom-call(bf16[64,512]{1,0:T(8,128)(2,1)} %tq.1, bf16[64,64]{1,0:T(8,128)(2,1)} %lq.1, bf16[64,512]{1,0:T(8,128)(2,1)} %hq.1, bf16[64,128]{1,0:T(8,128)(2,1)} %tk.1, bf16[64,64]{1,0:T(8,128)(2,1)} %lk.1, bf16[64,128]{1,0:T(8,128)(2,1)} %hk.1, bf16[64,128]{1,0:T(8,128)(2,1)} %tv.1, bf16[64,64]{1,0:T(8,128)(2,1)} %lv.1, ...), custom_call_target="tpu_custom_call" | custom-call | tf_op jit(solution)/shard_map/merge/pallas_call | solution.py:148
  7.3 2.4 %collective-permute-done.1.second = bf16[8,128]{1,0:T(8,128)(2,1)S(1)} collective-permute-done((bf16[8,128]{1,0:T(8,128)(2,1)S(1)}, bf16[8,128]{1,0:T(8,128)(2,1)S(1)}, u32[]{:S(2)}, u32[]{:S(2)}) %collective-permute-start.1) | collective-permute-done | bytes 2080 | tf_op jit(solution)/shard_map/ppermute | solution.py:147
  9.6 0.3 collective-permute-done.first
  10.0 4.6 %collective-permute-start.3 = (bf16[392,128]{1,0:T(8,128)(2,1)S(1)}, bf16[392,128]{1,0:T(8,128)(2,1)S(1)}, u32[]{:S(2)}, u32[]{:S(2)}) collective-permute-start(bf16[392,128]{1,0:T(8,128)(2,1)S(1)} %gain.1.refs_0_), channel_id=1, source_target_pairs={{160,0},{168,8},{176,16},{184,24},{192,32},{200,40},{208,48},{216,... | collective-permute-start | bytes 301064 | tf_op jit(solution)/shard_map/ppermute | solution.py:48
  14.6 2.6 %collective-permute-start.4 = (bf16[392,128]{1,0:T(8,128)(2,1)S(1)}, bf16[392,128]{1,0:T(8,128)(2,1)S(1)}, u32[]{:S(2)}, u32[]{:S(2)}) collective-permute-start(bf16[392,128]{1,0:T(8,128)(2,1)S(1)} %gain.1.refs_0_), channel_id=1, source_target_pairs={{80,0},{88,8},{64,16},{72,24},{112,32},{120,40},{96,48},{104,56},{... | collective-permute-start | bytes 301064 | tf_op jit(solution)/shard_map/ppermute | solution.py:48
  17.2 3.4 %collective-permute-done.3.refs_1_.refs_0_ = bf16[392,128]{1,0:T(8,128)(2,1)S(1)} collective-permute-done((bf16[392,128]{1,0:T(8,128)(2,1)S(1)}, bf16[392,128]{1,0:T(8,128)(2,1)S(1)}, u32[]{:S(2)}, u32[]{:S(2)}) %collective-permute-start.3) | collective-permute-done | bytes 100384 | tf_op jit(solution)/shard_map/ppermute | solution.py:48
  20.6 3.1 %collective-permute-start.8 = (bf16[784,128]{1,0:T(8,128)(2,1)S(1)}, bf16[784,128]{1,0:T(8,128)(2,1)S(1)}, u32[]{:S(2)}, u32[]{:S(2)}) collective-permute-start(bf16[784,128]{1,0:T(8,128)(2,1)S(1)} %pack.8), channel_id=1, source_target_pairs={{224,0},{232,8},{240,16},{248,24},{0,32},{8,40},{16,48},{24,56},{3... | collective-permute-start | bytes 602120 | tf_op jit(solution)/shard_map/ppermute | solution.py:48
  23.7 0.3 collective-permute-start.6
  24.0 0.6 %collective-permute-start.9 = (bf16[1176,128]{1,0:T(8,128)(2,1)S(1)}, bf16[1176,128]{1,0:T(8,128)(2,1)S(1)}, u32[]{:S(2)}, u32[]{:S(2)}) collective-permute-start(bf16[1176,128]{1,0:T(8,128)(2,1)S(1)} %pack.9), channel_id=1, source_target_pairs={{24,0},{0,8},{8,16},{16,24},{56,32},{32,40},{40,48},{48,56},{88,64... | collective-permute-start | bytes 903176 | tf_op jit(solution)/shard_map/ppermute | solution.py:48
  24.5 1.5 %collective-permute-start.7 = (bf16[392,128]{1,0:T(8,128)(2,1)S(1)}, bf16[392,128]{1,0:T(8,128)(2,1)S(1)}, u32[]{:S(2)}, u32[]{:S(2)}) collective-permute-start(bf16[392,128]{1,0:T(8,128)(2,1)S(1)} %gain.1.refs_0_), channel_id=1, source_target_pairs={{8,0},{16,8},{24,16},{0,24},{40,32},{48,40},{56,48},{32,56},{72,64... | collective-permute-start | bytes 301064 | tf_op jit(solution)/shard_map/ppermute | solution.py:48
  26.1 5.8 %collective-permute-start.5 = (bf16[392,128]{1,0:T(8,128)(2,1)S(1)}, bf16[392,128]{1,0:T(8,128)(2,1)S(1)}, u32[]{:S(2)}, u32[]{:S(2)}) collective-permute-start(bf16[392,128]{1,0:T(8,128)(2,1)S(1)} %gain.1.refs_0_), channel_id=1, source_target_pairs={{208,0},{216,8},{192,16},{200,24},{240,32},{248,40},{224,48},{232,... | collective-permute-start | bytes 301064 | tf_op jit(solution)/shard_map/ppermute | solution.py:48
  31.9 0.1 collective-permute-start.10
  32.0 3.7 %collective-permute-done.5.refs_2_.refs_1_.refs_0_.refs_3_ = bf16[392,128]{1,0:T(8,128)(2,1)S(1)} collective-permute-done((bf16[392,128]{1,0:T(8,128)(2,1)S(1)}, bf16[392,128]{1,0:T(8,128)(2,1)S(1)}, u32[]{:S(2)}, u32[]{:S(2)}) %collective-permute-start.5) | collective-permute-done | bytes 100384 | tf_op jit(solution)/shard_map/ppermute | solution.py:48
  35.8 3.4 %collective-permute-start.12 = (bf16[1960,128]{1,0:T(8,128)(2,1)S(1)}, bf16[1960,128]{1,0:T(8,128)(2,1)S(1)}, u32[]{:S(2)}, u32[]{:S(2)}) collective-permute-start(bf16[1960,128]{1,0:T(8,128)(2,1)S(1)} %pack.12), channel_id=1, source_target_pairs={{224,0},{232,8},{240,16},{248,24},{0,32},{8,40},{16,48},{24,56},{3... | collective-permute-start | bytes 1505288 | tf_op jit(solution)/shard_map/ppermute | solution.py:48
  39.3 3.3 %collective-permute-start.13 = (bf16[1568,128]{1,0:T(8,128)(2,1)S(1)}, bf16[1568,128]{1,0:T(8,128)(2,1)S(1)}, u32[]{:S(2)}, u32[]{:S(2)}) collective-permute-start(bf16[1568,128]{1,0:T(8,128)(2,1)S(1)} %pack.13), channel_id=1, source_target_pairs={{24,0},{0,8},{8,16},{16,24},{56,32},{32,40},{40,48},{48,56},{88,64... | collective-permute-start | bytes 1204232 | tf_op jit(solution)/shard_map/ppermute | solution.py:48
  42.6 0.1 collective-permute-start.14
  42.8 6.5 %collective-permute-done.11.refs_9_ = bf16[1568,128]{1,0:T(8,128)(2,1)S(1)} collective-permute-done((bf16[1568,128]{1,0:T(8,128)(2,1)S(1)}, bf16[1568,128]{1,0:T(8,128)(2,1)S(1)}, u32[]{:S(2)}, u32[]{:S(2)}) %collective-permute-start.11) | collective-permute-done | bytes 401440 | tf_op jit(solution)/shard_map/ppermute | solution.py:48
  49.3 2.7 %collective-permute-done.15.refs_13_ = bf16[976,128]{1,0:T(8,128)(2,1)S(1)} collective-permute-done((bf16[976,128]{1,0:T(8,128)(2,1)S(1)}, bf16[976,128]{1,0:T(8,128)(2,1)S(1)}, u32[]{:S(2)}, u32[]{:S(2)}) %collective-permute-start.15) | collective-permute-done | bytes 249888 | tf_op jit(solution)/shard_map/ppermute | solution.py:48
  52.0 2.6 %place.1 = (bf16[512,2048]{1,0:T(8,128)(2,1)}, bf16[128,2048]{1,0:T(8,128)(2,1)}, bf16[128,2048]{1,0:T(8,128)(2,1)}, bf16[16,128]{1,0:T(8,128)(2,1)}) custom-call(bf16[392,128]{1,0:T(8,128)(2,1)S(1)} %gain.1.refs_0_, bf16[392,128]{1,0:T(8,128)(2,1)S(1)} %collective-permute-done.3.refs_1_.refs_0_, ...), custom_call_target="tpu_custom_call" | custom-call | tf_op jit(solution)/shard_map/place/pallas_call | solution.py:180
  (25 shorter events, 0.4 us)
Async XLA Ops:
  1.5 5.8 %collective-permute-start.2 = (bf16[8,128]{1,0:T(8,128)(2,1)S(1)}, bf16[8,128]{1,0:T(8,128)(2,1)S(1)}, u32[]{:S(2)}, u32[]{:S(2)}) collective-permute-start(bf16[8,128]{1,0:T(8,128)(2,1)S(1)} %fusion.2.own), channel_id=1, source_target_pairs={{0,6},{2,0},{4,2},{6,4},{1,7},{3,1},{5,3},{7,5},{8,14},{10,8},{12,... | collective-permute-start | bytes 6152 | tf_op jit(solution)/shard_map/ppermute | solution.py:147
  4.5 5.1 %collective-permute-start.1 = (bf16[8,128]{1,0:T(8,128)(2,1)S(1)}, bf16[8,128]{1,0:T(8,128)(2,1)S(1)}, u32[]{:S(2)}, u32[]{:S(2)}) collective-permute-start(bf16[8,128]{1,0:T(8,128)(2,1)S(1)} %fusion.2.own), channel_id=1, source_target_pairs={{0,4},{2,6},{4,0},{6,2},{1,5},{3,7},{5,1},{7,3},{8,12},{10,14},{12... | collective-permute-start | bytes 6152 | tf_op jit(solution)/shard_map/ppermute | solution.py:147
  5.2 4.8 %collective-permute-start = (bf16[8,128]{1,0:T(8,128)(2,1)S(1)}, bf16[8,128]{1,0:T(8,128)(2,1)S(1)}, u32[]{:S(2)}, u32[]{:S(2)}) collective-permute-start(bf16[8,128]{1,0:T(8,128)(2,1)S(1)} %fusion.2.own), channel_id=1, source_target_pairs={{0,2},{2,4},{4,6},{6,0},{1,3},{3,5},{5,7},{7,1},{8,10},{10,12},{12... | collective-permute-start | bytes 6152 | tf_op jit(solution)/shard_map/ppermute | solution.py:147
  10.0 10.6 %collective-permute-start.3 = (bf16[392,128]{1,0:T(8,128)(2,1)S(1)}, bf16[392,128]{1,0:T(8,128)(2,1)S(1)}, u32[]{:S(2)}, u32[]{:S(2)}) collective-permute-start(bf16[392,128]{1,0:T(8,128)(2,1)S(1)} %gain.1.refs_0_), channel_id=1, source_target_pairs={{160,0},{168,8},{176,16},{184,24},{192,32},{200,40},{208,48},{216,... | collective-permute-start | bytes 301064 | tf_op jit(solution)/shard_map/ppermute | solution.py:48
  14.6 9.4 %collective-permute-start.4 = (bf16[392,128]{1,0:T(8,128)(2,1)S(1)}, bf16[392,128]{1,0:T(8,128)(2,1)S(1)}, u32[]{:S(2)}, u32[]{:S(2)}) collective-permute-start(bf16[392,128]{1,0:T(8,128)(2,1)S(1)} %gain.1.refs_0_), channel_id=1, source_target_pairs={{80,0},{88,8},{64,16},{72,24},{112,32},{120,40},{96,48},{104,56},{... | collective-permute-start | bytes 301064 | tf_op jit(solution)/shard_map/ppermute | solution.py:48
  20.6 15.1 %collective-permute-start.8 = (bf16[784,128]{1,0:T(8,128)(2,1)S(1)}, bf16[784,128]{1,0:T(8,128)(2,1)S(1)}, u32[]{:S(2)}, u32[]{:S(2)}) collective-permute-start(bf16[784,128]{1,0:T(8,128)(2,1)S(1)} %pack.8), channel_id=1, source_target_pairs={{224,0},{232,8},{240,16},{248,24},{0,32},{8,40},{16,48},{24,56},{3... | collective-permute-start | bytes 602120 | tf_op jit(solution)/shard_map/ppermute | solution.py:48
  23.7 8.2 %collective-permute-start.6 = (bf16[392,128]{1,0:T(8,128)(2,1)S(1)}, bf16[392,128]{1,0:T(8,128)(2,1)S(1)}, u32[]{:S(2)}, u32[]{:S(2)}) collective-permute-start(bf16[392,128]{1,0:T(8,128)(2,1)S(1)} %gain.1.refs_0_), channel_id=1, source_target_pairs={{32,0},{40,8},{48,16},{56,24},{64,32},{72,40},{80,48},{88,56},{96,... | collective-permute-start | bytes 301064 | tf_op jit(solution)/shard_map/ppermute | solution.py:48
  24.0 18.6 %collective-permute-start.9 = (bf16[1176,128]{1,0:T(8,128)(2,1)S(1)}, bf16[1176,128]{1,0:T(8,128)(2,1)S(1)}, u32[]{:S(2)}, u32[]{:S(2)}) collective-permute-start(bf16[1176,128]{1,0:T(8,128)(2,1)S(1)} %pack.9), channel_id=1, source_target_pairs={{24,0},{0,8},{8,16},{16,24},{56,32},{32,40},{40,48},{48,56},{88,64... | collective-permute-start | bytes 903176 | tf_op jit(solution)/shard_map/ppermute | solution.py:48
  24.5 7.5 %collective-permute-start.7 = (bf16[392,128]{1,0:T(8,128)(2,1)S(1)}, bf16[392,128]{1,0:T(8,128)(2,1)S(1)}, u32[]{:S(2)}, u32[]{:S(2)}) collective-permute-start(bf16[392,128]{1,0:T(8,128)(2,1)S(1)} %gain.1.refs_0_), channel_id=1, source_target_pairs={{8,0},{16,8},{24,16},{0,24},{40,32},{48,40},{56,48},{32,56},{72,64... | collective-permute-start | bytes 301064 | tf_op jit(solution)/shard_map/ppermute | solution.py:48
  26.1 9.6 %collective-permute-start.5 = (bf16[392,128]{1,0:T(8,128)(2,1)S(1)}, bf16[392,128]{1,0:T(8,128)(2,1)S(1)}, u32[]{:S(2)}, u32[]{:S(2)}) collective-permute-start(bf16[392,128]{1,0:T(8,128)(2,1)S(1)} %gain.1.refs_0_), channel_id=1, source_target_pairs={{208,0},{216,8},{192,16},{200,24},{240,32},{248,40},{224,48},{232,... | collective-permute-start | bytes 301064 | tf_op jit(solution)/shard_map/ppermute | solution.py:48
  31.9 10.6 %collective-permute-start.10 = (bf16[784,128]{1,0:T(8,128)(2,1)S(1)}, bf16[784,128]{1,0:T(8,128)(2,1)S(1)}, u32[]{:S(2)}, u32[]{:S(2)}) collective-permute-start(bf16[784,128]{1,0:T(8,128)(2,1)S(1)} %pack.10), channel_id=1, source_target_pairs={{32,0},{40,8},{48,16},{56,24},{64,32},{72,40},{80,48},{88,56},{96,... | collective-permute-start | bytes 602120 | tf_op jit(solution)/shard_map/ppermute | solution.py:48
  35.8 16.2 %collective-permute-start.12 = (bf16[1960,128]{1,0:T(8,128)(2,1)S(1)}, bf16[1960,128]{1,0:T(8,128)(2,1)S(1)}, u32[]{:S(2)}, u32[]{:S(2)}) collective-permute-start(bf16[1960,128]{1,0:T(8,128)(2,1)S(1)} %pack.12), channel_id=1, source_target_pairs={{224,0},{232,8},{240,16},{248,24},{0,32},{8,40},{16,48},{24,56},{3... | collective-permute-start | bytes 1505288 | tf_op jit(solution)/shard_map/ppermute | solution.py:48
  39.1 10.1 %collective-permute-start.11 = (bf16[1568,128]{1,0:T(8,128)(2,1)S(1)}, bf16[1568,128]{1,0:T(8,128)(2,1)S(1)}, u32[]{:S(2)}, u32[]{:S(2)}) collective-permute-start(bf16[1568,128]{1,0:T(8,128)(2,1)S(1)} %pack.11), channel_id=1, source_target_pairs={{8,0},{16,8},{24,16},{0,24},{40,32},{48,40},{56,48},{32,56},{72,64... | collective-permute-start | bytes 1204232 | tf_op jit(solution)/shard_map/ppermute | solution.py:48
  39.3 12.7 %collective-permute-start.13 = (bf16[1568,128]{1,0:T(8,128)(2,1)S(1)}, bf16[1568,128]{1,0:T(8,128)(2,1)S(1)}, u32[]{:S(2)}, u32[]{:S(2)}) collective-permute-start(bf16[1568,128]{1,0:T(8,128)(2,1)S(1)} %pack.13), channel_id=1, source_target_pairs={{24,0},{0,8},{8,16},{16,24},{56,32},{32,40},{40,48},{48,56},{88,64... | collective-permute-start | bytes 1204232 | tf_op jit(solution)/shard_map/ppermute | solution.py:48
  42.6 9.3 %collective-permute-start.14 = (bf16[1376,128]{1,0:T(8,128)(2,1)S(1)}, bf16[1376,128]{1,0:T(8,128)(2,1)S(1)}, u32[]{:S(2)}, u32[]{:S(2)}) collective-permute-start(bf16[1376,128]{1,0:T(8,128)(2,1)S(1)} %pack.14), channel_id=1, source_target_pairs={{32,0},{40,8},{48,16},{56,24},{64,32},{72,40},{80,48},{88,56},{96,... | collective-permute-start | bytes 1056776 | tf_op jit(solution)/shard_map/ppermute | solution.py:48
  42.7 9.2 %collective-permute-start.15 = (bf16[976,128]{1,0:T(8,128)(2,1)S(1)}, bf16[976,128]{1,0:T(8,128)(2,1)S(1)}, u32[]{:S(2)}, u32[]{:S(2)}) collective-permute-start(bf16[976,128]{1,0:T(8,128)(2,1)S(1)} %pack.15), channel_id=1, source_target_pairs={{8,0},{16,8},{24,16},{0,24},{40,32},{48,40},{56,48},{32,56},{72,64... | collective-permute-start | bytes 749576 | tf_op jit(solution)/shard_map/ppermute | solution.py:48

commit v4 on v3

--- a/solution.py
+++ b/solution.py
@@ -107,14 +107,21 @@
             if first <= chunk < last:
                 at = row + (chunk - first) * BLOCK
                 rows[chunk, pl.ds(pl.multiple_of(rank * BLOCK, BLOCK), BLOCK), :] = block[at : at + BLOCK, :]
-        for tile in range(RANKS * BLOCK // LANES):
-            lanes = slice(tile * LANES, (tile + 1) * LANES)
-            turned[chunk, :, lanes] = rows[chunk, lanes, :].T
         out, row = ((query, chunk), (key, chunk - 4), (value, chunk - 5))[max(0, chunk - 3)]
-        copies.append(
-            pltpu.make_async_copy(turned.at[chunk], out.at[row * LANES : (row + 1) * LANES, :], sems.at[chunk])
-        )
-        copies[-1].start()
+        half = RANKS * BLOCK // 2
+        for part in range(2):
+            for tile in range(half // LANES):
+                lanes = slice(part * half + tile * LANES, part * half + (tile + 1) * LANES)
+                turned[chunk, :, lanes] = rows[chunk, lanes, :].T
+            lanes = slice(part * half, (part + 1) * half)
+            copies.append(
+                pltpu.make_async_copy(
+                    turned.at[chunk, :, lanes],
+                    out.at[row * LANES : (row + 1) * LANES, lanes],
+                    sems.at[2 * chunk + part],
+                )
+            )
+            copies[-1].start()
     for block, row, first, last, rank in placed:
         if last == CHUNKS:
             at = row + (last - first) * BLOCK
@@ -191,7 +198,7 @@
             pltpu.VMEM((CHUNKS, width, LANES), bf16),
             pltpu.VMEM((RANKS, 8, LANES), jnp.float32),
             pltpu.VMEM((CHUNKS, LANES, width), bf16),
-            pltpu.SemaphoreType.DMA((CHUNKS,)),
+            pltpu.SemaphoreType.DMA((2 * CHUNKS,)),
         ],
         compiler_params=pltpu.CompilerParams(vmem_limit_bytes=16 * 2**20),
         name="place",

time: 54.7 us -> 54.7 us (level)
  no operation moved by 1% of the time
where the time goes in v4:
time: 54.7 us; the launch traced here: 54.6 us
  starting transfers between devices  30.1 us (55%)
  waiting for transfers between devices  19 us (35%)
  Pallas kernels  3.9 us (7%)
  between operations  0.77 us (1%)
  other arithmetic  0.71 us (1%)
    ppermute x13, starting transfers between devices, from_offset(): return lax.ppermute(array, ROWS, pairs)  25.4 us
    ppermute x13, waiting for transfers between devices, from_offset(): return lax.ppermute(array, ROWS, pairs)  16.3 us
    ppermute x3, starting transfers between devices, shards(): lax.ppermute(gain, 'tp', [(i, (i + s) % TP) for i in range(TP)])  4.69 us
    ppermute x3, waiting for transfers between devices, shards(): lax.ppermute(gain, 'tp', [(i, (i + s) % TP) for i in range(TP)])  2.71 us
    pallas_call x1, Pallas kernels, shards(): pl.pallas_call(lambda *refs: place_kernel(pieces, *refs), out_shape=(jax....  2.61 us
    pallas_call x1, Pallas kernels, shards(): pl.pallas_call(merge_kernel, out_shape=pltpu.VMEM((SENT_ROWS, LANES), bf1...  1.1 us
  transfers between devices with their start and end apart: 16, of which 6 were waited for; matrix products, arithmetic and copies ran while one was open for 0% of the time, Pallas kernels for 2%

profile of v4, /device:TPU:6, one launch (start us, length us, event | category | flops | bytes accessed | tf_op | source)
XLA Modules:
  0.0 54.6 jit_solution(11301314423349827654)
XLA Ops:
  0.7 0.7 %add_convert_fusion = bf16[16]{0:T(256)(128)(2,1)S(1)} fusion(f32[16]{0:T(128)} %param.20, f32[16]{0:T(128)} %param.21), kind=kLoop, calls=%fused_computation.12 | loop fusion | flops 32 | bytes 160 | tf_op jit(solution)/shard_map/convert_element_type | solution.py:151
  1.3 0.1 broadcast_in_dim.14
  1.5 3.1 %collective-permute-start.2 = (bf16[8,128]{1,0:T(8,128)(2,1)S(1)}, bf16[8,128]{1,0:T(8,128)(2,1)S(1)}, u32[]{:S(2)}, u32[]{:S(2)}) collective-permute-start(bf16[8,128]{1,0:T(8,128)(2,1)S(1)} %fusion.2.own), channel_id=1, source_target_pairs={{0,6},{2,0},{4,2},{6,4},{1,7},{3,1},{5,3},{7,5},{8,14},{10,8},{12,... | collective-permute-start | bytes 6152 | tf_op jit(solution)/shard_map/ppermute | solution.py:154
  4.5 0.6 %collective-permute-start.1 = (bf16[8,128]{1,0:T(8,128)(2,1)S(1)}, bf16[8,128]{1,0:T(8,128)(2,1)S(1)}, u32[]{:S(2)}, u32[]{:S(2)}) collective-permute-start(bf16[8,128]{1,0:T(8,128)(2,1)S(1)} %fusion.2.own), channel_id=1, source_target_pairs={{0,4},{2,6},{4,0},{6,2},{1,5},{3,7},{5,1},{7,3},{8,12},{10,14},{12... | collective-permute-start | bytes 6152 | tf_op jit(solution)/shard_map/ppermute | solution.py:154
  5.2 1.0 %collective-permute-start = (bf16[8,128]{1,0:T(8,128)(2,1)S(1)}, bf16[8,128]{1,0:T(8,128)(2,1)S(1)}, u32[]{:S(2)}, u32[]{:S(2)}) collective-permute-start(bf16[8,128]{1,0:T(8,128)(2,1)S(1)} %fusion.2.own), channel_id=1, source_target_pairs={{0,2},{2,4},{4,6},{6,0},{1,3},{3,5},{5,7},{7,1},{8,10},{10,12},{12... | collective-permute-start | bytes 6152 | tf_op jit(solution)/shard_map/ppermute | solution.py:154
  6.1 1.1 %merge.1._ = bf16[392,128]{1,0:T(8,128)(2,1)S(1)} custom-call(bf16[64,512]{1,0:T(8,128)(2,1)} %tq.1, bf16[64,64]{1,0:T(8,128)(2,1)} %lq.1, bf16[64,512]{1,0:T(8,128)(2,1)} %hq.1, bf16[64,128]{1,0:T(8,128)(2,1)} %tk.1, bf16[64,64]{1,0:T(8,128)(2,1)} %lk.1, bf16[64,128]{1,0:T(8,128)(2,1)} %hk.1, bf16[64,128]{1,0:T(8,128)(2,1)} %tv.1, bf16[64,64]{1,0:T(8,128)(2,1)} %lv.1, ...), custom_call_target="tpu_custom_call" | custom-call | tf_op jit(solution)/shard_map/merge/pallas_call | solution.py:155
  7.3 2.4 %collective-permute-done.1.second = bf16[8,128]{1,0:T(8,128)(2,1)S(1)} collective-permute-done((bf16[8,128]{1,0:T(8,128)(2,1)S(1)}, bf16[8,128]{1,0:T(8,128)(2,1)S(1)}, u32[]{:S(2)}, u32[]{:S(2)}) %collective-permute-start.1) | collective-permute-done | bytes 2080 | tf_op jit(solution)/shard_map/ppermute | solution.py:154
  9.6 0.3 collective-permute-done.first
  10.0 4.6 %collective-permute-start.3 = (bf16[392,128]{1,0:T(8,128)(2,1)S(1)}, bf16[392,128]{1,0:T(8,128)(2,1)S(1)}, u32[]{:S(2)}, u32[]{:S(2)}) collective-permute-start(bf16[392,128]{1,0:T(8,128)(2,1)S(1)} %gain.1.refs_0_), channel_id=1, source_target_pairs={{160,0},{168,8},{176,16},{184,24},{192,32},{200,40},{208,48},{216,... | collective-permute-start | bytes 301064 | tf_op jit(solution)/shard_map/ppermute | solution.py:48
  14.6 2.6 %collective-permute-start.4 = (bf16[392,128]{1,0:T(8,128)(2,1)S(1)}, bf16[392,128]{1,0:T(8,128)(2,1)S(1)}, u32[]{:S(2)}, u32[]{:S(2)}) collective-permute-start(bf16[392,128]{1,0:T(8,128)(2,1)S(1)} %gain.1.refs_0_), channel_id=1, source_target_pairs={{80,0},{88,8},{64,16},{72,24},{112,32},{120,40},{96,48},{104,56},{... | collective-permute-start | bytes 301064 | tf_op jit(solution)/shard_map/ppermute | solution.py:48
  17.2 3.4 %collective-permute-done.3.refs_1_.refs_0_ = bf16[392,128]{1,0:T(8,128)(2,1)S(1)} collective-permute-done((bf16[392,128]{1,0:T(8,128)(2,1)S(1)}, bf16[392,128]{1,0:T(8,128)(2,1)S(1)}, u32[]{:S(2)}, u32[]{:S(2)}) %collective-permute-start.3) | collective-permute-done | bytes 100384 | tf_op jit(solution)/shard_map/ppermute | solution.py:48
  20.6 3.1 %collective-permute-start.8 = (bf16[784,128]{1,0:T(8,128)(2,1)S(1)}, bf16[784,128]{1,0:T(8,128)(2,1)S(1)}, u32[]{:S(2)}, u32[]{:S(2)}) collective-permute-start(bf16[784,128]{1,0:T(8,128)(2,1)S(1)} %pack.8), channel_id=1, source_target_pairs={{224,0},{232,8},{240,16},{248,24},{0,32},{8,40},{16,48},{24,56},{3... | collective-permute-start | bytes 602120 | tf_op jit(solution)/shard_map/ppermute | solution.py:48
  23.7 0.3 collective-permute-start.6
  24.0 0.6 %collective-permute-start.9 = (bf16[1176,128]{1,0:T(8,128)(2,1)S(1)}, bf16[1176,128]{1,0:T(8,128)(2,1)S(1)}, u32[]{:S(2)}, u32[]{:S(2)}) collective-permute-start(bf16[1176,128]{1,0:T(8,128)(2,1)S(1)} %pack.9), channel_id=1, source_target_pairs={{24,0},{0,8},{8,16},{16,24},{56,32},{32,40},{40,48},{48,56},{88,64... | collective-permute-start | bytes 903176 | tf_op jit(solution)/shard_map/ppermute | solution.py:48
  24.5 1.5 %collective-permute-start.7 = (bf16[392,128]{1,0:T(8,128)(2,1)S(1)}, bf16[392,128]{1,0:T(8,128)(2,1)S(1)}, u32[]{:S(2)}, u32[]{:S(2)}) collective-permute-start(bf16[392,128]{1,0:T(8,128)(2,1)S(1)} %gain.1.refs_0_), channel_id=1, source_target_pairs={{8,0},{16,8},{24,16},{0,24},{40,32},{48,40},{56,48},{32,56},{72,64... | collective-permute-start | bytes 301064 | tf_op jit(solution)/shard_map/ppermute | solution.py:48
  26.1 5.8 %collective-permute-start.5 = (bf16[392,128]{1,0:T(8,128)(2,1)S(1)}, bf16[392,128]{1,0:T(8,128)(2,1)S(1)}, u32[]{:S(2)}, u32[]{:S(2)}) collective-permute-start(bf16[392,128]{1,0:T(8,128)(2,1)S(1)} %gain.1.refs_0_), channel_id=1, source_target_pairs={{208,0},{216,8},{192,16},{200,24},{240,32},{248,40},{224,48},{232,... | collective-permute-start | bytes 301064 | tf_op jit(solution)/shard_map/ppermute | solution.py:48
  31.9 0.1 collective-permute-start.10
  32.0 3.7 %collective-permute-done.5.refs_2_.refs_1_.refs_0_.refs_3_ = bf16[392,128]{1,0:T(8,128)(2,1)S(1)} collective-permute-done((bf16[392,128]{1,0:T(8,128)(2,1)S(1)}, bf16[392,128]{1,0:T(8,128)(2,1)S(1)}, u32[]{:S(2)}, u32[]{:S(2)}) %collective-permute-start.5) | collective-permute-done | bytes 100384 | tf_op jit(solution)/shard_map/ppermute | solution.py:48
  35.8 3.4 %collective-permute-start.12 = (bf16[1960,128]{1,0:T(8,128)(2,1)S(1)}, bf16[1960,128]{1,0:T(8,128)(2,1)S(1)}, u32[]{:S(2)}, u32[]{:S(2)}) collective-permute-start(bf16[1960,128]{1,0:T(8,128)(2,1)S(1)} %pack.12), channel_id=1, source_target_pairs={{224,0},{232,8},{240,16},{248,24},{0,32},{8,40},{16,48},{24,56},{3... | collective-permute-start | bytes 1505288 | tf_op jit(solution)/shard_map/ppermute | solution.py:48
  39.3 3.3 %collective-permute-start.13 = (bf16[1568,128]{1,0:T(8,128)(2,1)S(1)}, bf16[1568,128]{1,0:T(8,128)(2,1)S(1)}, u32[]{:S(2)}, u32[]{:S(2)}) collective-permute-start(bf16[1568,128]{1,0:T(8,128)(2,1)S(1)} %pack.13), channel_id=1, source_target_pairs={{24,0},{0,8},{8,16},{16,24},{56,32},{32,40},{40,48},{48,56},{88,64... | collective-permute-start | bytes 1204232 | tf_op jit(solution)/shard_map/ppermute | solution.py:48
  42.6 0.1 collective-permute-start.14
  42.8 6.5 %collective-permute-done.11.refs_9_ = bf16[1568,128]{1,0:T(8,128)(2,1)S(1)} collective-permute-done((bf16[1568,128]{1,0:T(8,128)(2,1)S(1)}, bf16[1568,128]{1,0:T(8,128)(2,1)S(1)}, u32[]{:S(2)}, u32[]{:S(2)}) %collective-permute-start.11) | collective-permute-done | bytes 401440 | tf_op jit(solution)/shard_map/ppermute | solution.py:48
  49.3 2.7 %collective-permute-done.15.refs_13_ = bf16[976,128]{1,0:T(8,128)(2,1)S(1)} collective-permute-done((bf16[976,128]{1,0:T(8,128)(2,1)S(1)}, bf16[976,128]{1,0:T(8,128)(2,1)S(1)}, u32[]{:S(2)}, u32[]{:S(2)}) %collective-permute-start.15) | collective-permute-done | bytes 249888 | tf_op jit(solution)/shard_map/ppermute | solution.py:48
  52.0 2.6 %place.1 = (bf16[512,2048]{1,0:T(8,128)(2,1)}, bf16[128,2048]{1,0:T(8,128)(2,1)}, bf16[128,2048]{1,0:T(8,128)(2,1)}, bf16[16,128]{1,0:T(8,128)(2,1)}) custom-call(bf16[392,128]{1,0:T(8,128)(2,1)S(1)} %gain.1.refs_0_, bf16[392,128]{1,0:T(8,128)(2,1)S(1)} %collective-permute-done.3.refs_1_.refs_0_, ...), custom_call_target="tpu_custom_call" | custom-call | tf_op jit(solution)/shard_map/place/pallas_call | solution.py:187
  (25 shorter events, 0.4 us)
Async XLA Ops:
  1.5 5.8 %collective-permute-start.2 = (bf16[8,128]{1,0:T(8,128)(2,1)S(1)}, bf16[8,128]{1,0:T(8,128)(2,1)S(1)}, u32[]{:S(2)}, u32[]{:S(2)}) collective-permute-start(bf16[8,128]{1,0:T(8,128)(2,1)S(1)} %fusion.2.own), channel_id=1, source_target_pairs={{0,6},{2,0},{4,2},{6,4},{1,7},{3,1},{5,3},{7,5},{8,14},{10,8},{12,... | collective-permute-start | bytes 6152 | tf_op jit(solution)/shard_map/ppermute | solution.py:154
  4.5 5.1 %collective-permute-start.1 = (bf16[8,128]{1,0:T(8,128)(2,1)S(1)}, bf16[8,128]{1,0:T(8,128)(2,1)S(1)}, u32[]{:S(2)}, u32[]{:S(2)}) collective-permute-start(bf16[8,128]{1,0:T(8,128)(2,1)S(1)} %fusion.2.own), channel_id=1, source_target_pairs={{0,4},{2,6},{4,0},{6,2},{1,5},{3,7},{5,1},{7,3},{8,12},{10,14},{12... | collective-permute-start | bytes 6152 | tf_op jit(solution)/shard_map/ppermute | solution.py:154
  5.2 4.8 %collective-permute-start = (bf16[8,128]{1,0:T(8,128)(2,1)S(1)}, bf16[8,128]{1,0:T(8,128)(2,1)S(1)}, u32[]{:S(2)}, u32[]{:S(2)}) collective-permute-start(bf16[8,128]{1,0:T(8,128)(2,1)S(1)} %fusion.2.own), channel_id=1, source_target_pairs={{0,2},{2,4},{4,6},{6,0},{1,3},{3,5},{5,7},{7,1},{8,10},{10,12},{12... | collective-permute-start | bytes 6152 | tf_op jit(solution)/shard_map/ppermute | solution.py:154
  10.0 10.6 %collective-permute-start.3 = (bf16[392,128]{1,0:T(8,128)(2,1)S(1)}, bf16[392,128]{1,0:T(8,128)(2,1)S(1)}, u32[]{:S(2)}, u32[]{:S(2)}) collective-permute-start(bf16[392,128]{1,0:T(8,128)(2,1)S(1)} %gain.1.refs_0_), channel_id=1, source_target_pairs={{160,0},{168,8},{176,16},{184,24},{192,32},{200,40},{208,48},{216,... | collective-permute-start | bytes 301064 | tf_op jit(solution)/shard_map/ppermute | solution.py:48
  14.6 9.4 %collective-permute-start.4 = (bf16[392,128]{1,0:T(8,128)(2,1)S(1)}, bf16[392,128]{1,0:T(8,128)(2,1)S(1)}, u32[]{:S(2)}, u32[]{:S(2)}) collective-permute-start(bf16[392,128]{1,0:T(8,128)(2,1)S(1)} %gain.1.refs_0_), channel_id=1, source_target_pairs={{80,0},{88,8},{64,16},{72,24},{112,32},{120,40},{96,48},{104,56},{... | collective-permute-start | bytes 301064 | tf_op jit(solution)/shard_map/ppermute | solution.py:48
  20.6 15.1 %collective-permute-start.8 = (bf16[784,128]{1,0:T(8,128)(2,1)S(1)}, bf16[784,128]{1,0:T(8,128)(2,1)S(1)}, u32[]{:S(2)}, u32[]{:S(2)}) collective-permute-start(bf16[784,128]{1,0:T(8,128)(2,1)S(1)} %pack.8), channel_id=1, source_target_pairs={{224,0},{232,8},{240,16},{248,24},{0,32},{8,40},{16,48},{24,56},{3... | collective-permute-start | bytes 602120 | tf_op jit(solution)/shard_map/ppermute | solution.py:48
  23.7 8.2 %collective-permute-start.6 = (bf16[392,128]{1,0:T(8,128)(2,1)S(1)}, bf16[392,128]{1,0:T(8,128)(2,1)S(1)}, u32[]{:S(2)}, u32[]{:S(2)}) collective-permute-start(bf16[392,128]{1,0:T(8,128)(2,1)S(1)} %gain.1.refs_0_), channel_id=1, source_target_pairs={{32,0},{40,8},{48,16},{56,24},{64,32},{72,40},{80,48},{88,56},{96,... | collective-permute-start | bytes 301064 | tf_op jit(solution)/shard_map/ppermute | solution.py:48
  24.0 18.6 %collective-permute-start.9 = (bf16[1176,128]{1,0:T(8,128)(2,1)S(1)}, bf16[1176,128]{1,0:T(8,128)(2,1)S(1)}, u32[]{:S(2)}, u32[]{:S(2)}) collective-permute-start(bf16[1176,128]{1,0:T(8,128)(2,1)S(1)} %pack.9), channel_id=1, source_target_pairs={{24,0},{0,8},{8,16},{16,24},{56,32},{32,40},{40,48},{48,56},{88,64... | collective-permute-start | bytes 903176 | tf_op jit(solution)/shard_map/ppermute | solution.py:48
  24.5 7.5 %collective-permute-start.7 = (bf16[392,128]{1,0:T(8,128)(2,1)S(1)}, bf16[392,128]{1,0:T(8,128)(2,1)S(1)}, u32[]{:S(2)}, u32[]{:S(2)}) collective-permute-start(bf16[392,128]{1,0:T(8,128)(2,1)S(1)} %gain.1.refs_0_), channel_id=1, source_target_pairs={{8,0},{16,8},{24,16},{0,24},{40,32},{48,40},{56,48},{32,56},{72,64... | collective-permute-start | bytes 301064 | tf_op jit(solution)/shard_map/ppermute | solution.py:48
  26.1 9.6 %collective-permute-start.5 = (bf16[392,128]{1,0:T(8,128)(2,1)S(1)}, bf16[392,128]{1,0:T(8,128)(2,1)S(1)}, u32[]{:S(2)}, u32[]{:S(2)}) collective-permute-start(bf16[392,128]{1,0:T(8,128)(2,1)S(1)} %gain.1.refs_0_), channel_id=1, source_target_pairs={{208,0},{216,8},{192,16},{200,24},{240,32},{248,40},{224,48},{232,... | collective-permute-start | bytes 301064 | tf_op jit(solution)/shard_map/ppermute | solution.py:48
  31.9 10.6 %collective-permute-start.10 = (bf16[784,128]{1,0:T(8,128)(2,1)S(1)}, bf16[784,128]{1,0:T(8,128)(2,1)S(1)}, u32[]{:S(2)}, u32[]{:S(2)}) collective-permute-start(bf16[784,128]{1,0:T(8,128)(2,1)S(1)} %pack.10), channel_id=1, source_target_pairs={{32,0},{40,8},{48,16},{56,24},{64,32},{72,40},{80,48},{88,56},{96,... | collective-permute-start | bytes 602120 | tf_op jit(solution)/shard_map/ppermute | solution.py:48
  35.8 16.2 %collective-permute-start.12 = (bf16[1960,128]{1,0:T(8,128)(2,1)S(1)}, bf16[1960,128]{1,0:T(8,128)(2,1)S(1)}, u32[]{:S(2)}, u32[]{:S(2)}) collective-permute-start(bf16[1960,128]{1,0:T(8,128)(2,1)S(1)} %pack.12), channel_id=1, source_target_pairs={{224,0},{232,8},{240,16},{248,24},{0,32},{8,40},{16,48},{24,56},{3... | collective-permute-start | bytes 1505288 | tf_op jit(solution)/shard_map/ppermute | solution.py:48
  39.1 10.1 %collective-permute-start.11 = (bf16[1568,128]{1,0:T(8,128)(2,1)S(1)}, bf16[1568,128]{1,0:T(8,128)(2,1)S(1)}, u32[]{:S(2)}, u32[]{:S(2)}) collective-permute-start(bf16[1568,128]{1,0:T(8,128)(2,1)S(1)} %pack.11), channel_id=1, source_target_pairs={{8,0},{16,8},{24,16},{0,24},{40,32},{48,40},{56,48},{32,56},{72,64... | collective-permute-start | bytes 1204232 | tf_op jit(solution)/shard_map/ppermute | solution.py:48
  39.3 12.7 %collective-permute-start.13 = (bf16[1568,128]{1,0:T(8,128)(2,1)S(1)}, bf16[1568,128]{1,0:T(8,128)(2,1)S(1)}, u32[]{:S(2)}, u32[]{:S(2)}) collective-permute-start(bf16[1568,128]{1,0:T(8,128)(2,1)S(1)} %pack.13), channel_id=1, source_target_pairs={{24,0},{0,8},{8,16},{16,24},{56,32},{32,40},{40,48},{48,56},{88,64... | collective-permute-start | bytes 1204232 | tf_op jit(solution)/shard_map/ppermute | solution.py:48
  42.6 9.3 %collective-permute-start.14 = (bf16[1376,128]{1,0:T(8,128)(2,1)S(1)}, bf16[1376,128]{1,0:T(8,128)(2,1)S(1)}, u32[]{:S(2)}, u32[]{:S(2)}) collective-permute-start(bf16[1376,128]{1,0:T(8,128)(2,1)S(1)} %pack.14), channel_id=1, source_target_pairs={{32,0},{40,8},{48,16},{56,24},{64,32},{72,40},{80,48},{88,56},{96,... | collective-permute-start | bytes 1056776 | tf_op jit(solution)/shard_map/ppermute | solution.py:48
  42.7 9.2 %collective-permute-start.15 = (bf16[976,128]{1,0:T(8,128)(2,1)S(1)}, bf16[976,128]{1,0:T(8,128)(2,1)S(1)}, u32[]{:S(2)}, u32[]{:S(2)}) collective-permute-start(bf16[976,128]{1,0:T(8,128)(2,1)S(1)} %pack.15), channel_id=1, source_target_pairs={{8,0},{16,8},{24,16},{0,24},{40,32},{48,40},{56,48},{32,56},{72,64... | collective-permute-start | bytes 749576 | tf_op jit(solution)/shard_map/ppermute | solution.py:48
